TPU v7x, 32 devices: a whole 2x2x4 slice. The times are simulated.
32 devices in a mesh: dp: 4 (over x, y), sp: 8 (over z, core).
Axes of the slice: x: 2, y: 2, z: 4, core: 2. Of those that a mesh axis runs over, the one named last changes fastest.
Arguments:
- x: bfloat16 [4, 16384, 128], P('dp', 'sp'), parts along dimension 0
- w_in: bfloat16 [14, 3, 128, 256], replicated
- w_res: bfloat16 [14, 128, 128], replicated
- w_skip: bfloat16 [14, 128, 128], replicated
Outputs:
- output 1: float32 [4, 16384, 128], P('dp', 'sp'), parts along dimension 0
- output 2: float32 [4, 16384, 128], P('dp', 'sp'), parts along dimension 0
There are 4 independent parts. A program takes and returns all parts, laid end to end along the dimension named above; an argument that names none is the same for every part.
All inputs are finite; a program needn't handle non-finite values.
Results may differ from a plain program's by a relative error of at most 0.00526473.
Values are sent between devices in bfloat16 or wider.
A program may use at most 1 GiB of HBM per device.

v0:
```python
import jax
import jax.numpy as jnp
from jax import lax
from jax.sharding import PartitionSpec as P


def neighbour_taps(cur_bf, dilation, n_dev):
    n_rows = cur_bf.shape[1]
    if dilation < n_rows:
        from_prev = lax.ppermute(cur_bf[:, n_rows - dilation:], 'sp', [(src, src + 1) for src in range(n_dev - 1)])
        from_next = lax.ppermute(cur_bf[:, :dilation], 'sp', [(src + 1, src) for src in range(n_dev - 1)])
        left_tap = jnp.concatenate([from_prev, cur_bf[:, :n_rows - dilation]], axis=1)
        right_tap = jnp.concatenate([cur_bf[:, dilation:], from_next], axis=1)
    else:
        n_hops = dilation // n_rows
        left_tap = lax.ppermute(cur_bf, 'sp', [(src, src + n_hops) for src in range(n_dev - n_hops)])
        right_tap = lax.ppermute(cur_bf, 'sp', [(src + n_hops, src) for src in range(n_dev - n_hops)])
    return left_tap, right_tap


def solution(mesh):
    n_dev = mesh.shape['sp']
    act_spec = P('dp', 'sp', None)

    def local_stack(x_local, w_in, w_res, w_skip):
        n_chan = x_local.shape[2]
        residual = x_local.astype(jnp.float32)
        skip_sum = jnp.zeros(x_local.shape[:2] + (w_skip.shape[2],), jnp.float32)
        for layer in range(w_in.shape[0]):
            cur_bf = residual.astype(jnp.bfloat16)
            left_tap, right_tap = neighbour_taps(cur_bf, 2 ** layer, n_dev)
            pre_act = (jnp.einsum('bsc,cf->bsf', left_tap, w_in[layer, 0], preferred_element_type=jnp.float32)
                       + jnp.einsum('bsc,cf->bsf', cur_bf, w_in[layer, 1], preferred_element_type=jnp.float32)
                       + jnp.einsum('bsc,cf->bsf', right_tap, w_in[layer, 2], preferred_element_type=jnp.float32))
            gated = (jnp.tanh(pre_act[..., :n_chan]) * jax.nn.sigmoid(pre_act[..., n_chan:])).astype(jnp.bfloat16)
            residual = residual + jnp.einsum('bsc,cf->bsf', gated, w_res[layer], preferred_element_type=jnp.float32)
            skip_sum = skip_sum + jnp.einsum('bsc,cf->bsf', gated, w_skip[layer], preferred_element_type=jnp.float32)
        return residual, skip_sum

    return jax.shard_map(local_stack, mesh=mesh, in_specs=(act_spec, P(), P(), P()), out_specs=(act_spec, act_spec), check_vma=False)
```

profile of v0, /device:TPU:0, one launch (start us, length us, event | category | flops | bytes accessed | tf_op | source)
XLA Modules:
  0.0 169.9 jit_solution(10073564946038885044)
XLA Ops:
  0.6 0.8 fusion.415
  1.4 2.4 %collective-permute-start = (bf16[1,1,128]{2,1,0:T(2,128)(2,1)S(1)}, bf16[1,1,128]{2,1,0:T(2,128)(2,1)S(1)}, u32[]{:S(2)}, u32[]{:S(2)}) collective-permute-start(bf16[1,1,128]{2,1,0:T(2,128)(2,1)S(1)} %get-tuple-element.40), channel_id=1, source_target_pairs={{0,1},{1,2},{2,3},{3,4},{4,5},{5,6},{6,7},{8,9},{9,10},{10,11},{11... | collective-permute-start | bytes 776 | tf_op jit(solution)/shard_map/ppermute | solution.py:10
  3.8 1.6 collective-permute-start.1
  5.4 1.5 fusion.416
  6.9 1.3 fusion.232
  8.1 1.2 collective-permute-done.1
  9.8 0.4 fusion.27
  10.2 0.4 fusion.99
  10.6 0.6 copy-done.2
  12.2 1.3 collective-permute-start.3
  13.8 4.9 %collective-permute-start.2 = (bf16[1,2,128]{2,1,0:T(2,128)(2,1)S(1)}, bf16[1,2,128]{2,1,0:T(2,128)(2,1)S(1)}, u32[]{:S(2)}, u32[]{:S(2)}) collective-permute-start(bf16[1,2,128]{2,1,0:T(2,128)(2,1)S(1)} %get-tuple-element.36), channel_id=1, source_target_pairs={{0,1},{1,2},{2,3},{3,4},{4,5},{5,6},{6,7},{8,9},{9,10},{10,11},{11... | collective-permute-start | bytes 1544 | tf_op jit(solution)/shard_map/ppermute | solution.py:10
  19.4 0.4 fusion.25
  19.9 0.4 fusion.100
  21.2 1.3 collective-permute-start.5
  22.8 4.2 %collective-permute-start.4 = (bf16[1,4,128]{2,1,0:T(4,128)(2,1)S(1)}, bf16[1,4,128]{2,1,0:T(4,128)(2,1)S(1)}, u32[]{:S(2)}, u32[]{:S(2)}) collective-permute-start(bf16[1,4,128]{2,1,0:T(4,128)(2,1)S(1)} %get-tuple-element.32), channel_id=1, source_target_pairs={{0,1},{1,2},{2,3},{3,4},{4,5},{5,6},{6,7},{8,9},{9,10},{10,11},{11... | collective-permute-start | bytes 3080 | tf_op jit(solution)/shard_map/ppermute | solution.py:10
  27.8 0.4 fusion.23
  29.5 1.3 collective-permute-start.7
  31.1 4.7 %collective-permute-start.6 = (bf16[1,8,128]{2,1,0:T(8,128)(2,1)S(1)}, bf16[1,8,128]{2,1,0:T(8,128)(2,1)S(1)}, u32[]{:S(2)}, u32[]{:S(2)}) collective-permute-start(bf16[1,8,128]{2,1,0:T(8,128)(2,1)S(1)} %get-tuple-element.28), channel_id=1, source_target_pairs={{0,1},{1,2},{2,3},{3,4},{4,5},{5,6},{6,7},{8,9},{9,10},{10,11},{11... | collective-permute-start | bytes 6152 | tf_op jit(solution)/shard_map/ppermute | solution.py:10
  38.2 1.3 collective-permute-start.9
  39.8 4.7 %collective-permute-start.8 = (bf16[1,16,128]{2,1,0:T(8,128)(2,1)S(1)}, bf16[1,16,128]{2,1,0:T(8,128)(2,1)S(1)}, u32[]{:S(2)}, u32[]{:S(2)}) collective-permute-start(bf16[1,16,128]{2,1,0:T(8,128)(2,1)S(1)} %get-tuple-element.24), channel_id=1, source_target_pairs={{0,1},{1,2},{2,3},{3,4},{4,5},{5,6},{6,7},{8,9},{9,10},{10,11},{11... | collective-permute-start | bytes 12296 | tf_op jit(solution)/shard_map/ppermute | solution.py:10
  46.9 1.3 collective-permute-start.11
  48.5 4.9 %collective-permute-start.10 = (bf16[1,32,128]{2,1,0:T(8,128)(2,1)S(1)}, bf16[1,32,128]{2,1,0:T(8,128)(2,1)S(1)}, u32[]{:S(2)}, u32[]{:S(2)}) collective-permute-start(bf16[1,32,128]{2,1,0:T(8,128)(2,1)S(1)} %get-tuple-element.20), channel_id=1, source_target_pairs={{0,1},{1,2},{2,3},{3,4},{4,5},{5,6},{6,7},{8,9},{9,10},{10,11},{11... | collective-permute-start | bytes 24584 | tf_op jit(solution)/shard_map/ppermute | solution.py:10
  54.1 0.4 fusion.17
  55.8 1.3 collective-permute-start.13
  57.4 4.8 %collective-permute-start.12 = (bf16[1,64,128]{2,1,0:T(8,128)(2,1)S(1)}, bf16[1,64,128]{2,1,0:T(8,128)(2,1)S(1)}, u32[]{:S(2)}, u32[]{:S(2)}) collective-permute-start(bf16[1,64,128]{2,1,0:T(8,128)(2,1)S(1)} %get-tuple-element.16), channel_id=1, source_target_pairs={{0,1},{1,2},{2,3},{3,4},{4,5},{5,6},{6,7},{8,9},{9,10},{10,11},{11... | collective-permute-start | bytes 49160 | tf_op jit(solution)/shard_map/ppermute | solution.py:10
  64.6 1.3 collective-permute-start.15
  66.2 4.8 %collective-permute-start.14 = (bf16[1,128,128]{2,1,0:T(8,128)(2,1)S(1)}, bf16[1,128,128]{2,1,0:T(8,128)(2,1)S(1)}, u32[]{:S(2)}, u32[]{:S(2)}) collective-permute-start(bf16[1,128,128]{2,1,0:T(8,128)(2,1)S(1)} %get-tuple-element.12), channel_id=1, source_target_pairs={{0,1},{1,2},{2,3},{3,4},{4,5},{5,6},{6,7},{8,9},{9,10},{10,11},{11... | collective-permute-start | bytes 98312 | tf_op jit(solution)/shard_map/ppermute | solution.py:10
  73.5 1.3 collective-permute-start.17
  75.1 5.0 %collective-permute-start.16 = (bf16[1,256,128]{2,1,0:T(8,128)(2,1)S(1)}, bf16[1,256,128]{2,1,0:T(8,128)(2,1)S(1)}, u32[]{:S(2)}, u32[]{:S(2)}) collective-permute-start(bf16[1,256,128]{2,1,0:T(8,128)(2,1)S(1)} %get-tuple-element.8), channel_id=1, source_target_pairs={{0,1},{1,2},{2,3},{3,4},{4,5},{5,6},{6,7},{8,9},{9,10},{10,11},{11... | collective-permute-start | bytes 196616 | tf_op jit(solution)/shard_map/ppermute | solution.py:10
  80.5 0.5 collective-permute-done.16
  82.6 1.3 collective-permute-start.19
  84.2 5.3 %collective-permute-start.18 = (bf16[1,512,128]{2,1,0:T(8,128)(2,1)S(1)}, bf16[1,512,128]{2,1,0:T(8,128)(2,1)S(1)}, u32[]{:S(2)}, u32[]{:S(2)}) collective-permute-start(bf16[1,512,128]{2,1,0:T(8,128)(2,1)S(1)} %get-tuple-element.4), channel_id=1, source_target_pairs={{0,1},{1,2},{2,3},{3,4},{4,5},{5,6},{6,7},{8,9},{9,10},{10,11},{11... | collective-permute-start | bytes 393224 | tf_op jit(solution)/shard_map/ppermute | solution.py:10
  89.9 0.5 collective-permute-done.18
  92.1 5.2 %collective-permute-start.20 = (bf16[1,1024,128]{2,1,0:T(8,128)(2,1)S(1)}, bf16[1,1024,128]{2,1,0:T(8,128)(2,1)S(1)}, u32[]{:S(2)}, u32[]{:S(2)}) collective-permute-start(bf16[1,1024,128]{2,1,0:T(8,128)(2,1)S(1)} %get-tuple-element.2), channel_id=1, source_target_pairs={{0,1},{1,2},{2,3},{3,4},{4,5},{5,6},{6,7},{8,9},{9,10},{10,11},{11... | collective-permute-start | bytes 786440 | tf_op jit(solution)/shard_map/ppermute | solution.py:10
  97.3 1.3 collective-permute-start.21
  98.9 3.8 %collective-permute-done.21 = bf16[1,1024,128]{2,1,0:T(8,128)(2,1)S(1)} collective-permute-done((bf16[1,1024,128]{2,1,0:T(8,128)(2,1)S(1)}, bf16[1,1024,128]{2,1,0:T(8,128)(2,1)S(1)}, u32[]{:S(2)}, u32[]{:S(2)}) %collective-permute-start.21) | collective-permute-done | bytes 262176 | tf_op jit(solution)/shard_map/ppermute | solution.py:11
  104.2 1.3 collective-permute-start.23
  105.5 7.5 %collective-permute-start.22 = (bf16[1,2048,128]{2,1,0:T(8,128)(2,1)S(1)}, bf16[1,2048,128]{2,1,0:T(8,128)(2,1)S(1)}, u32[]{:S(2)}, u32[]{:S(2)}) collective-permute-start(bf16[1,2048,128]{2,1,0:T(8,128)(2,1)S(1)} %get-tuple-element.64), channel_id=1, source_target_pairs={{0,1},{1,2},{2,3},{3,4},{4,5},{5,6},{6,7},{8,9},{9,10},{10,11},{11... | collective-permute-start | bytes 1572872 | tf_op jit(solution)/shard_map/ppermute | solution.py:16
  115.5 1.3 collective-permute-start.25
  116.8 11.3 %collective-permute-start.24 = (bf16[1,2048,128]{2,1,0:T(8,128)(2,1)S(1)}, bf16[1,2048,128]{2,1,0:T(8,128)(2,1)S(1)}, u32[]{:S(2)}, u32[]{:S(2)}) collective-permute-start(bf16[1,2048,128]{2,1,0:T(8,128)(2,1)S(1)} %get-tuple-element.66), channel_id=1, source_target_pairs={{0,2},{1,3},{2,4},{3,5},{4,6},{5,7},{8,10},{9,11},{10,12},{11,13},... | collective-permute-start | bytes 1572872 | tf_op jit(solution)/shard_map/ppermute | solution.py:16
  128.7 8.8 %collective-permute-done.25 = bf16[1,2048,128]{2,1,0:T(8,128)(2,1)S(1)} collective-permute-done((bf16[1,2048,128]{2,1,0:T(8,128)(2,1)S(1)}, bf16[1,2048,128]{2,1,0:T(8,128)(2,1)S(1)}, u32[]{:S(2)}, u32[]{:S(2)}) %collective-permute-start.25) | collective-permute-done | bytes 524320 | tf_op jit(solution)/shard_map/ppermute | solution.py:17
  137.9 0.8 collective-permute-done.24
  139.8 1.3 collective-permute-start.27
  141.1 5.5 %collective-permute-start.26 = (bf16[1,2048,128]{2,1,0:T(8,128)(2,1)S(1)}, bf16[1,2048,128]{2,1,0:T(8,128)(2,1)S(1)}, u32[]{:S(2)}, u32[]{:S(2)}) collective-permute-start(bf16[1,2048,128]{2,1,0:T(8,128)(2,1)S(1)} %get-tuple-element.68), channel_id=1, source_target_pairs={{0,4},{1,5},{2,6},{3,7},{8,12},{9,13},{10,14},{11,15},{16,20},{17,... | collective-permute-start | bytes 1572872 | tf_op jit(solution)/shard_map/ppermute | solution.py:16
  147.3 18.8 %collective-permute-done.27 = bf16[1,2048,128]{2,1,0:T(8,128)(2,1)S(1)} collective-permute-done((bf16[1,2048,128]{2,1,0:T(8,128)(2,1)S(1)}, bf16[1,2048,128]{2,1,0:T(8,128)(2,1)S(1)}, u32[]{:S(2)}, u32[]{:S(2)}) %collective-permute-start.27) | collective-permute-done | bytes 524320 | tf_op jit(solution)/shard_map/ppermute | solution.py:17
  166.6 0.4 fusion.1
  167.4 1.3 fusion.28
  168.7 1.2 fusion.42
  (121 shorter events, 30.9 us)
Async XLA Ops:
  0.6 6.2 %copy-start = (bf16[1,2048,128]{2,1,0:T(8,128)(2,1)S(1)}, bf16[1,2048,128]{2,1,0:T(8,128)(2,1)}, u32[]{:S(2)}) copy-start(bf16[1,2048,128]{2,1,0:T(8,128)(2,1)} %param.4) | copy-start | bytes 1572868
  1.4 8.4 %collective-permute-start = (bf16[1,1,128]{2,1,0:T(2,128)(2,1)S(1)}, bf16[1,1,128]{2,1,0:T(2,128)(2,1)S(1)}, u32[]{:S(2)}, u32[]{:S(2)}) collective-permute-start(bf16[1,1,128]{2,1,0:T(2,128)(2,1)S(1)} %get-tuple-element.40), channel_id=1, source_target_pairs={{0,1},{1,2},{2,3},{3,4},{4,5},{5,6},{6,7},{8,9},{9,10},{10,11},{11... | collective-permute-start | bytes 776 | tf_op jit(solution)/shard_map/ppermute | solution.py:10
  3.8 5.5 %copy-start.1 = (bf16[14,3,128,256]{3,2,1,0:T(8,128)(2,1)S(1)}, bf16[14,3,128,256]{3,2,1,0:T(8,128)(2,1)}, u32[]{:S(2)}) copy-start(bf16[14,3,128,256]{3,2,1,0:T(8,128)(2,1)} %param.5) | copy-start | bytes 8257540
  3.8 5.5 %collective-permute-start.1 = (bf16[1,1,128]{2,1,0:T(2,128)(2,1)S(1)}, bf16[1,1,128]{2,1,0:T(2,128)(2,1)S(1)}, u32[]{:S(2)}, u32[]{:S(2)}) collective-permute-start(bf16[1,1,128]{2,1,0:T(2,128)(2,1)S(1)} %get-tuple-element.41), channel_id=1, source_target_pairs={{1,0},{2,1},{3,2},{4,3},{5,4},{6,5},{7,6},{9,8},{10,9},{11,10},{12... | collective-permute-start | bytes 776 | tf_op jit(solution)/shard_map/ppermute | solution.py:11
  10.2 1.0 copy-start.2
  11.5 1.9 %copy-start.3 = (bf16[14,128,128]{2,1,0:T(8,128)(2,1)S(1)}, bf16[14,128,128]{2,1,0:T(8,128)(2,1)}, u32[]{:S(2)}) copy-start(bf16[14,128,128]{2,1,0:T(8,128)(2,1)} %param.7) | copy-start | bytes 1376260
  12.2 6.5 %collective-permute-start.3 = (bf16[1,2,128]{2,1,0:T(2,128)(2,1)S(1)}, bf16[1,2,128]{2,1,0:T(2,128)(2,1)S(1)}, u32[]{:S(2)}, u32[]{:S(2)}) collective-permute-start(bf16[1,2,128]{2,1,0:T(2,128)(2,1)S(1)} %get-tuple-element.37), channel_id=1, source_target_pairs={{1,0},{2,1},{3,2},{4,3},{5,4},{6,5},{7,6},{9,8},{10,9},{11,10},{12... | collective-permute-start | bytes 1544 | tf_op jit(solution)/shard_map/ppermute | solution.py:11
  13.8 5.7 %collective-permute-start.2 = (bf16[1,2,128]{2,1,0:T(2,128)(2,1)S(1)}, bf16[1,2,128]{2,1,0:T(2,128)(2,1)S(1)}, u32[]{:S(2)}, u32[]{:S(2)}) collective-permute-start(bf16[1,2,128]{2,1,0:T(2,128)(2,1)S(1)} %get-tuple-element.36), channel_id=1, source_target_pairs={{0,1},{1,2},{2,3},{3,4},{4,5},{5,6},{6,7},{8,9},{9,10},{10,11},{11... | collective-permute-start | bytes 1544 | tf_op jit(solution)/shard_map/ppermute | solution.py:10
  21.2 5.8 %collective-permute-start.5 = (bf16[1,4,128]{2,1,0:T(4,128)(2,1)S(1)}, bf16[1,4,128]{2,1,0:T(4,128)(2,1)S(1)}, u32[]{:S(2)}, u32[]{:S(2)}) collective-permute-start(bf16[1,4,128]{2,1,0:T(4,128)(2,1)S(1)} %get-tuple-element.33), channel_id=1, source_target_pairs={{1,0},{2,1},{3,2},{4,3},{5,4},{6,5},{7,6},{9,8},{10,9},{11,10},{12... | collective-permute-start | bytes 3080 | tf_op jit(solution)/shard_map/ppermute | solution.py:11
  22.8 5.0 %collective-permute-start.4 = (bf16[1,4,128]{2,1,0:T(4,128)(2,1)S(1)}, bf16[1,4,128]{2,1,0:T(4,128)(2,1)S(1)}, u32[]{:S(2)}, u32[]{:S(2)}) collective-permute-start(bf16[1,4,128]{2,1,0:T(4,128)(2,1)S(1)} %get-tuple-element.32), channel_id=1, source_target_pairs={{0,1},{1,2},{2,3},{3,4},{4,5},{5,6},{6,7},{8,9},{9,10},{10,11},{11... | collective-permute-start | bytes 3080 | tf_op jit(solution)/shard_map/ppermute | solution.py:10
  29.5 6.3 %collective-permute-start.7 = (bf16[1,8,128]{2,1,0:T(8,128)(2,1)S(1)}, bf16[1,8,128]{2,1,0:T(8,128)(2,1)S(1)}, u32[]{:S(2)}, u32[]{:S(2)}) collective-permute-start(bf16[1,8,128]{2,1,0:T(8,128)(2,1)S(1)} %get-tuple-element.29), channel_id=1, source_target_pairs={{1,0},{2,1},{3,2},{4,3},{5,4},{6,5},{7,6},{9,8},{10,9},{11,10},{12... | collective-permute-start | bytes 6152 | tf_op jit(solution)/shard_map/ppermute | solution.py:11
  31.1 5.5 %collective-permute-start.6 = (bf16[1,8,128]{2,1,0:T(8,128)(2,1)S(1)}, bf16[1,8,128]{2,1,0:T(8,128)(2,1)S(1)}, u32[]{:S(2)}, u32[]{:S(2)}) collective-permute-start(bf16[1,8,128]{2,1,0:T(8,128)(2,1)S(1)} %get-tuple-element.28), channel_id=1, source_target_pairs={{0,1},{1,2},{2,3},{3,4},{4,5},{5,6},{6,7},{8,9},{9,10},{10,11},{11... | collective-permute-start | bytes 6152 | tf_op jit(solution)/shard_map/ppermute | solution.py:10
  38.2 6.3 %collective-permute-start.9 = (bf16[1,16,128]{2,1,0:T(8,128)(2,1)S(1)}, bf16[1,16,128]{2,1,0:T(8,128)(2,1)S(1)}, u32[]{:S(2)}, u32[]{:S(2)}) collective-permute-start(bf16[1,16,128]{2,1,0:T(8,128)(2,1)S(1)} %get-tuple-element.25), channel_id=1, source_target_pairs={{1,0},{2,1},{3,2},{4,3},{5,4},{6,5},{7,6},{9,8},{10,9},{11,10},{12... | collective-permute-start | bytes 12296 | tf_op jit(solution)/shard_map/ppermute | solution.py:11
  39.8 5.5 %collective-permute-start.8 = (bf16[1,16,128]{2,1,0:T(8,128)(2,1)S(1)}, bf16[1,16,128]{2,1,0:T(8,128)(2,1)S(1)}, u32[]{:S(2)}, u32[]{:S(2)}) collective-permute-start(bf16[1,16,128]{2,1,0:T(8,128)(2,1)S(1)} %get-tuple-element.24), channel_id=1, source_target_pairs={{0,1},{1,2},{2,3},{3,4},{4,5},{5,6},{6,7},{8,9},{9,10},{10,11},{11... | collective-permute-start | bytes 12296 | tf_op jit(solution)/shard_map/ppermute | solution.py:10
  46.9 6.5 %collective-permute-start.11 = (bf16[1,32,128]{2,1,0:T(8,128)(2,1)S(1)}, bf16[1,32,128]{2,1,0:T(8,128)(2,1)S(1)}, u32[]{:S(2)}, u32[]{:S(2)}) collective-permute-start(bf16[1,32,128]{2,1,0:T(8,128)(2,1)S(1)} %get-tuple-element.21), channel_id=1, source_target_pairs={{1,0},{2,1},{3,2},{4,3},{5,4},{6,5},{7,6},{9,8},{10,9},{11,10},{12... | collective-permute-start | bytes 24584 | tf_op jit(solution)/shard_map/ppermute | solution.py:11
  48.5 5.6 %collective-permute-start.10 = (bf16[1,32,128]{2,1,0:T(8,128)(2,1)S(1)}, bf16[1,32,128]{2,1,0:T(8,128)(2,1)S(1)}, u32[]{:S(2)}, u32[]{:S(2)}) collective-permute-start(bf16[1,32,128]{2,1,0:T(8,128)(2,1)S(1)} %get-tuple-element.20), channel_id=1, source_target_pairs={{0,1},{1,2},{2,3},{3,4},{4,5},{5,6},{6,7},{8,9},{9,10},{10,11},{11... | collective-permute-start | bytes 24584 | tf_op jit(solution)/shard_map/ppermute | solution.py:10
  55.8 6.4 %collective-permute-start.13 = (bf16[1,64,128]{2,1,0:T(8,128)(2,1)S(1)}, bf16[1,64,128]{2,1,0:T(8,128)(2,1)S(1)}, u32[]{:S(2)}, u32[]{:S(2)}) collective-permute-start(bf16[1,64,128]{2,1,0:T(8,128)(2,1)S(1)} %get-tuple-element.17), channel_id=1, source_target_pairs={{1,0},{2,1},{3,2},{4,3},{5,4},{6,5},{7,6},{9,8},{10,9},{11,10},{12... | collective-permute-start | bytes 49160 | tf_op jit(solution)/shard_map/ppermute | solution.py:11
  57.4 5.6 %collective-permute-start.12 = (bf16[1,64,128]{2,1,0:T(8,128)(2,1)S(1)}, bf16[1,64,128]{2,1,0:T(8,128)(2,1)S(1)}, u32[]{:S(2)}, u32[]{:S(2)}) collective-permute-start(bf16[1,64,128]{2,1,0:T(8,128)(2,1)S(1)} %get-tuple-element.16), channel_id=1, source_target_pairs={{0,1},{1,2},{2,3},{3,4},{4,5},{5,6},{6,7},{8,9},{9,10},{10,11},{11... | collective-permute-start | bytes 49160 | tf_op jit(solution)/shard_map/ppermute | solution.py:10
  64.6 6.4 %collective-permute-start.15 = (bf16[1,128,128]{2,1,0:T(8,128)(2,1)S(1)}, bf16[1,128,128]{2,1,0:T(8,128)(2,1)S(1)}, u32[]{:S(2)}, u32[]{:S(2)}) collective-permute-start(bf16[1,128,128]{2,1,0:T(8,128)(2,1)S(1)} %get-tuple-element.13), channel_id=1, source_target_pairs={{1,0},{2,1},{3,2},{4,3},{5,4},{6,5},{7,6},{9,8},{10,9},{11,10},{12... | collective-permute-start | bytes 98312 | tf_op jit(solution)/shard_map/ppermute | solution.py:11
  66.2 5.7 %collective-permute-start.14 = (bf16[1,128,128]{2,1,0:T(8,128)(2,1)S(1)}, bf16[1,128,128]{2,1,0:T(8,128)(2,1)S(1)}, u32[]{:S(2)}, u32[]{:S(2)}) collective-permute-start(bf16[1,128,128]{2,1,0:T(8,128)(2,1)S(1)} %get-tuple-element.12), channel_id=1, source_target_pairs={{0,1},{1,2},{2,3},{3,4},{4,5},{5,6},{6,7},{8,9},{9,10},{10,11},{11... | collective-permute-start | bytes 98312 | tf_op jit(solution)/shard_map/ppermute | solution.py:10
  73.5 6.6 %collective-permute-start.17 = (bf16[1,256,128]{2,1,0:T(8,128)(2,1)S(1)}, bf16[1,256,128]{2,1,0:T(8,128)(2,1)S(1)}, u32[]{:S(2)}, u32[]{:S(2)}) collective-permute-start(bf16[1,256,128]{2,1,0:T(8,128)(2,1)S(1)} %get-tuple-element.9), channel_id=1, source_target_pairs={{1,0},{2,1},{3,2},{4,3},{5,4},{6,5},{7,6},{9,8},{10,9},{11,10},{12... | collective-permute-start | bytes 196616 | tf_op jit(solution)/shard_map/ppermute | solution.py:11
  75.1 5.9 %collective-permute-start.16 = (bf16[1,256,128]{2,1,0:T(8,128)(2,1)S(1)}, bf16[1,256,128]{2,1,0:T(8,128)(2,1)S(1)}, u32[]{:S(2)}, u32[]{:S(2)}) collective-permute-start(bf16[1,256,128]{2,1,0:T(8,128)(2,1)S(1)} %get-tuple-element.8), channel_id=1, source_target_pairs={{0,1},{1,2},{2,3},{3,4},{4,5},{5,6},{6,7},{8,9},{9,10},{10,11},{11... | collective-permute-start | bytes 196616 | tf_op jit(solution)/shard_map/ppermute | solution.py:10
  82.6 6.9 %collective-permute-start.19 = (bf16[1,512,128]{2,1,0:T(8,128)(2,1)S(1)}, bf16[1,512,128]{2,1,0:T(8,128)(2,1)S(1)}, u32[]{:S(2)}, u32[]{:S(2)}) collective-permute-start(bf16[1,512,128]{2,1,0:T(8,128)(2,1)S(1)} %get-tuple-element.5), channel_id=1, source_target_pairs={{1,0},{2,1},{3,2},{4,3},{5,4},{6,5},{7,6},{9,8},{10,9},{11,10},{12... | collective-permute-start | bytes 393224 | tf_op jit(solution)/shard_map/ppermute | solution.py:11
  84.2 6.3 %collective-permute-start.18 = (bf16[1,512,128]{2,1,0:T(8,128)(2,1)S(1)}, bf16[1,512,128]{2,1,0:T(8,128)(2,1)S(1)}, u32[]{:S(2)}, u32[]{:S(2)}) collective-permute-start(bf16[1,512,128]{2,1,0:T(8,128)(2,1)S(1)} %get-tuple-element.4), channel_id=1, source_target_pairs={{0,1},{1,2},{2,3},{3,4},{4,5},{5,6},{6,7},{8,9},{9,10},{10,11},{11... | collective-permute-start | bytes 393224 | tf_op jit(solution)/shard_map/ppermute | solution.py:10
  92.1 11.0 %collective-permute-start.20 = (bf16[1,1024,128]{2,1,0:T(8,128)(2,1)S(1)}, bf16[1,1024,128]{2,1,0:T(8,128)(2,1)S(1)}, u32[]{:S(2)}, u32[]{:S(2)}) collective-permute-start(bf16[1,1024,128]{2,1,0:T(8,128)(2,1)S(1)} %get-tuple-element.2), channel_id=1, source_target_pairs={{0,1},{1,2},{2,3},{3,4},{4,5},{5,6},{6,7},{8,9},{9,10},{10,11},{11... | collective-permute-start | bytes 786440 | tf_op jit(solution)/shard_map/ppermute | solution.py:10
  97.3 5.3 %collective-permute-start.21 = (bf16[1,1024,128]{2,1,0:T(8,128)(2,1)S(1)}, bf16[1,1024,128]{2,1,0:T(8,128)(2,1)S(1)}, u32[]{:S(2)}, u32[]{:S(2)}) collective-permute-start(bf16[1,1024,128]{2,1,0:T(8,128)(2,1)S(1)} %get-tuple-element.3), channel_id=1, source_target_pairs={{1,0},{2,1},{3,2},{4,3},{5,4},{6,5},{7,6},{9,8},{10,9},{11,10},{12... | collective-permute-start | bytes 786440 | tf_op jit(solution)/shard_map/ppermute | solution.py:11
  104.2 9.6 %collective-permute-start.23 = (bf16[1,2048,128]{2,1,0:T(8,128)(2,1)S(1)}, bf16[1,2048,128]{2,1,0:T(8,128)(2,1)S(1)}, u32[]{:S(2)}, u32[]{:S(2)}) collective-permute-start(bf16[1,2048,128]{2,1,0:T(8,128)(2,1)S(1)} %get-tuple-element.64), channel_id=1, source_target_pairs={{1,0},{2,1},{3,2},{4,3},{5,4},{6,5},{7,6},{9,8},{10,9},{11,10},{12... | collective-permute-start | bytes 1572872 | tf_op jit(solution)/shard_map/ppermute | solution.py:17
  105.5 8.8 %collective-permute-start.22 = (bf16[1,2048,128]{2,1,0:T(8,128)(2,1)S(1)}, bf16[1,2048,128]{2,1,0:T(8,128)(2,1)S(1)}, u32[]{:S(2)}, u32[]{:S(2)}) collective-permute-start(bf16[1,2048,128]{2,1,0:T(8,128)(2,1)S(1)} %get-tuple-element.64), channel_id=1, source_target_pairs={{0,1},{1,2},{2,3},{3,4},{4,5},{5,6},{6,7},{8,9},{9,10},{10,11},{11... | collective-permute-start | bytes 1572872 | tf_op jit(solution)/shard_map/ppermute | solution.py:16
  115.5 22.0 %collective-permute-start.25 = (bf16[1,2048,128]{2,1,0:T(8,128)(2,1)S(1)}, bf16[1,2048,128]{2,1,0:T(8,128)(2,1)S(1)}, u32[]{:S(2)}, u32[]{:S(2)}) collective-permute-start(bf16[1,2048,128]{2,1,0:T(8,128)(2,1)S(1)} %get-tuple-element.66), channel_id=1, source_target_pairs={{2,0},{3,1},{4,2},{5,3},{6,4},{7,5},{10,8},{11,9},{12,10},{13,11},... | collective-permute-start | bytes 1572872 | tf_op jit(solution)/shard_map/ppermute | solution.py:17
  116.8 21.9 %collective-permute-start.24 = (bf16[1,2048,128]{2,1,0:T(8,128)(2,1)S(1)}, bf16[1,2048,128]{2,1,0:T(8,128)(2,1)S(1)}, u32[]{:S(2)}, u32[]{:S(2)}) collective-permute-start(bf16[1,2048,128]{2,1,0:T(8,128)(2,1)S(1)} %get-tuple-element.66), channel_id=1, source_target_pairs={{0,2},{1,3},{2,4},{3,5},{4,6},{5,7},{8,10},{9,11},{10,12},{11,13},... | collective-permute-start | bytes 1572872 | tf_op jit(solution)/shard_map/ppermute | solution.py:16
  139.8 26.4 %collective-permute-start.27 = (bf16[1,2048,128]{2,1,0:T(8,128)(2,1)S(1)}, bf16[1,2048,128]{2,1,0:T(8,128)(2,1)S(1)}, u32[]{:S(2)}, u32[]{:S(2)}) collective-permute-start(bf16[1,2048,128]{2,1,0:T(8,128)(2,1)S(1)} %get-tuple-element.68), channel_id=1, source_target_pairs={{4,0},{5,1},{6,2},{7,3},{12,8},{13,9},{14,10},{15,11},{20,16},{21,... | collective-permute-start | bytes 1572872 | tf_op jit(solution)/shard_map/ppermute | solution.py:17
  141.1 25.5 %collective-permute-start.26 = (bf16[1,2048,128]{2,1,0:T(8,128)(2,1)S(1)}, bf16[1,2048,128]{2,1,0:T(8,128)(2,1)S(1)}, u32[]{:S(2)}, u32[]{:S(2)}) collective-permute-start(bf16[1,2048,128]{2,1,0:T(8,128)(2,1)S(1)} %get-tuple-element.68), channel_id=1, source_target_pairs={{0,4},{1,5},{2,6},{3,7},{8,12},{9,13},{10,14},{11,15},{16,20},{17,... | collective-permute-start | bytes 1572872 | tf_op jit(solution)/shard_map/ppermute | solution.py:16
where the time goes:
time: 171 us; the launch traced here: 170 us
  starting transfers between devices  93.6 us (55%)
  waiting for transfers between devices  37 us (22%)
  matrix products  28.1 us (16%)
  other arithmetic  5.86 us (3%)
  local copies, waits for them, and re-layouts  3.8 us (2%)
    ppermute x11, starting transfers between devices, neighbour_taps(): lax.ppermute(cur_bf[:, n_rows - dilation:], 'sp', [(src, src + 1) for src...  50.9 us
    ppermute x3, waiting for transfers between devices, neighbour_taps(): lax.ppermute(cur_bf, 'sp', [(src + n_hops, src) for src in range(n_dev -...  27.6 us
    ppermute x3, starting transfers between devices, neighbour_taps(): lax.ppermute(cur_bf, 'sp', [(src, src + n_hops) for src in range(n_dev -...  24.3 us
    ppermute x11, starting transfers between devices, neighbour_taps(): lax.ppermute(cur_bf[:, :dilation], 'sp', [(src + 1, src) for src in range...  14.5 us
    dot_general x14, matrix products, local_stack(): jnp.einsum('bsc,cf->bsf', cur_bf, w_in[layer, 1], preferred_element_type=...  6.63 us
    dot_general x14, matrix products, local_stack(): jnp.einsum('bsc,cf->bsf', left_tap, w_in[layer, 0], preferred_element_typ...  5.88 us
    convert_element_type x14, other arithmetic, local_stack(): (jnp.tanh(pre_act[..., :n_chan]) * jax.nn.sigmoid(pre_act[..., n_chan:]))...  5.86 us
    dot_general x14, matrix products, local_stack(): jnp.einsum('bsc,cf->bsf', right_tap, w_in[layer, 2], preferred_element_ty...  5.79 us
  transfers between devices with their start and end apart: 28, of which 15 were waited for; matrix products, arithmetic and copies ran while one was open for 8% of the time, Pallas kernels for 0%

commit v1 on v0

v1 whole, which is shorter than its diff:
```python
import functools

import jax
import jax.numpy as jnp
from jax import lax
from jax.experimental import pallas as pl
from jax.experimental.pallas import tpu as pltpu
from jax.sharding import PartitionSpec as P

MESH = pl.DeviceIdType.MESH
N_DEV = 8
ROWS = 2048
CH = 128
EXT = 256
PAD = EXT + 16
REACH = [256, 256, 256, 240, 224, 192, 128, 0]
CHUNK = 256
ORDER = [0, 1, 6, 7, 3, 4, 2, 5]


def kernel(x_ref, win_ref, wres_ref, wskip_ref, h_ref, s_ref,
           xb, ha, hb, sk, u4, u5, u6, u7, u8, u9, u10, u11, u12, u13,
           v11l, v11r, v12l, v12r, v13, win, wrs, lsem, wsem, osem, ssem, rsem):
    me = lax.axis_index('sp')
    has_l, has_r = me >= 1, me <= N_DEV - 2
    has_l2, has_r2 = me >= 2, me <= N_DEV - 3
    low = me < N_DEV // 2
    partner = jnp.where(low, me + N_DEV // 2, me - N_DEV // 2)
    have = {-1: has_l, 1: has_r, -2: has_l2, 2: has_r2}

    loads = []
    own_x = pltpu.make_async_copy(x_ref.at[0], xb.at[pl.ds(EXT, ROWS)], lsem)
    own_x.start()
    for k in range(14):
        trio = [pltpu.make_async_copy(win_ref.at[k], win.at[k], wsem.at[k, 0]),
                pltpu.make_async_copy(wres_ref.at[k], wrs.at[k, :, pl.ds(0, CH)], wsem.at[k, 1]),
                pltpu.make_async_copy(wskip_ref.at[k], wrs.at[k, :, pl.ds(CH, CH)], wsem.at[k, 2])]
        for c in trio:
            c.start()
        loads.append(trio)

    barrier = pltpu.get_barrier_semaphore()
    for dj, ok in have.items():
        @pl.when(ok)
        def _():
            pl.semaphore_signal(barrier, inc=1, device_id={'sp': me + dj}, device_id_type=MESH)
    pl.semaphore_signal(barrier, inc=1, device_id={'sp': partner}, device_id_type=MESH)

    def zero(ref, start, count):
        ref[pl.ds(start, count), :] = jnp.zeros((count, CH), ref.dtype)

    @pl.when(jnp.logical_not(has_l))
    def _():
        zero(xb, 0, EXT)
        zero(u8, 0, 256)
        zero(u9, 0, 512)
        zero(u10, 0, 1024)

    @pl.when(jnp.logical_not(has_r))
    def _():
        zero(xb, EXT + ROWS, EXT)
        zero(u8, 256 + ROWS, 256)
        zero(u9, 512 + ROWS, 512)
        zero(u10, 1024 + ROWS, 1024)
    for buf in (ha, hb):
        zero(buf, 0, 16)
        zero(buf, PAD + ROWS + EXT, 16)

    peers = 1
    for ok in have.values():
        peers += jnp.where(ok, 1, 0)
    pl.semaphore_wait(barrier, peers)

    count = [0]
    sent = []

    def remote(src, dst, dj):
        i = count[0]
        count[0] += 1
        dev = partner if dj is None else me + dj
        cp = pltpu.make_async_remote_copy(src_ref=src, dst_ref=dst, send_sem=ssem.at[i], recv_sem=rsem.at[i],
                                          device_id={'sp': dev}, device_id_type=MESH)
        if dj is None:
            cp.start()
        else:
            @pl.when(have[dj])
            def _():
                cp.start()
        sent.append((cp, dj))
        return cp, dj

    def arrived(copies):
        for cp, dj in copies:
            if dj is None:
                cp.wait_recv()
            else:
                @pl.when(have[-dj])
                def _():
                    cp.wait_recv()

    x_halo = [remote(x_ref.at[0, pl.ds(0, EXT)], xb.at[pl.ds(EXT + ROWS, EXT)], -1),
              remote(x_ref.at[0, pl.ds(ROWS - EXT, EXT)], xb.at[pl.ds(0, EXT)], 1)]

    u_ref = {4: (u4, EXT), 5: (u5, EXT), 6: (u6, EXT), 7: (u7, EXT), 8: (u8, 256), 9: (u9, 512), 10: (u10, 1024),
             11: (u11, 0), 12: (u12, 0), 13: (u13, 0)}

    def rows_of(ref, base, tile, shift):
        parts = [ref[pl.ds(base + r + shift, n), :] for r, n in tile]
        return parts[0] if len(parts) == 1 else jnp.concatenate(parts, axis=0)

    def state(k):
        if k < 4:
            return ((ha, hb), (hb, ha))[k % 2]
        return ha, ha

    def pre_act(k, tile, taps=None):
        d = 2 ** k
        if taps is not None:
            left, right = taps
            ref, base = u_ref[k]
            cur = rows_of(ref, base, tile, 0)
        elif k < 4:
            src = state(k)[0]
            left, cur, right = [rows_of(src, PAD, tile, o).astype(jnp.bfloat16) for o in (-d, 0, d)]
        else:
            ref, base = u_ref[k]
            left, cur, right = [rows_of(ref, base, tile, o) for o in (-d, 0, d)]
        return jnp.dot(jnp.concatenate([left, cur, right], axis=1), win[k], preferred_element_type=jnp.float32)

    def finish(k, tile, z):
        gate = jnp.tanh(z[:, :CH]) * jax.nn.sigmoid(z[:, CH:])
        pieces, off = [], 0
        for r, n in tile:
            g = gate[off:off + n]
            before, after = max(0, -r), max(0, r + n - ROWS)
            if before:
                g = jnp.concatenate([jnp.where(has_l, g[:before], 0.0), g[before:]], axis=0)
            if after:
                g = jnp.concatenate([g[:n - after], jnp.where(has_r, g[n - after:], 0.0)], axis=0)
            pieces.append(g)
            off += n
        gate = (pieces[0] if len(pieces) == 1 else jnp.concatenate(pieces, axis=0)).astype(jnp.bfloat16)
        y = jnp.dot(gate, wrs[k], preferred_element_type=jnp.float32)
        src, dst = state(k)
        off = 0
        for r, n in tile:
            new = src[pl.ds(PAD + r, n), :] + y[off:off + n, :CH]
            dst[pl.ds(PAD + r, n), :] = new
            if 4 <= k + 1 <= 13:
                ref, base = u_ref[k + 1]
                ref[pl.ds(base + r, n), :] = new.astype(jnp.bfloat16)
            lo, hi = max(r, 0), min(r + n, ROWS)
            part = y[off + lo - r:off + hi - r, CH:]
            if k == 0:
                sk[pl.ds(lo, hi - lo), :] = part
            else:
                sk[pl.ds(lo, hi - lo), :] += part
            off += n

    def run(k, tiles):
        z = {i: pre_act(k, tiles[i]) for i in range(min(2, len(tiles)))}
        for i in range(len(tiles)):
            if i + 2 < len(tiles):
                z[i + 2] = pre_act(k, tiles[i + 2])
            finish(k, tiles[i], z.pop(i))

    def weights(k):
        for c in loads[k]:
            c.wait()

    own_x.wait()
    arrived(x_halo)
    ha[pl.ds(16, ROWS + 2 * EXT), :] = xb[...].astype(jnp.float32)

    for k in range(7):
        weights(k)
        e = REACH[k]
        run(k, [[(-e, 256 + e)], [(256, 512)], [(768, 512)], [(1280, 512)], [(1792, 256 + e)]])
    weights(7)
    run(7, [[(0, 256), (1792, 256)]])
    c8 = [remote(u8.at[pl.ds(256, 256)], u8.at[pl.ds(256 + ROWS, 256)], -1),
          remote(u8.at[pl.ds(ROWS, 256)], u8.at[pl.ds(0, 256)], 1)]
    run(7, [[(256, 512)], [(768, 512)], [(1280, 512)]])

    def edge9(r):
        return remote(u9.at[pl.ds(512 + r, 256)], u9.at[pl.ds(512 + r + (ROWS if r < 512 else -ROWS), 256)], -1 if r < 512 else 1)

    weights(8)
    run(8, [[(256, 512)], [(768, 512)], [(1280, 512)]])
    c9a = [edge9(256), edge9(1536)]
    arrived(c8)
    run(8, [[(0, 256), (1792, 256)]])
    c9b = [edge9(0), edge9(1792)]

    def edge10(r, n):
        return remote(u10.at[pl.ds(1024 + r, n)], u10.at[pl.ds(1024 + r + (ROWS if r < 1024 else -ROWS), n)], -1 if r < 1024 else 1)

    weights(9)
    run(9, [[(512, 512)], [(1024, 512)]])
    c10a = [edge10(512, 512), edge10(1024, 512)]
    arrived(c9a)
    run(9, [[(0, 256), (1792, 256)]])
    c10b = [edge10(0, 256), edge10(1792, 256)]
    arrived(c9b)
    run(9, [[(256, 256), (1536, 256)]])
    c10c = [edge10(256, 256), edge10(1536, 256)]

    weights(10)
    c11 = {}

    def send11(chunks):
        for c in chunks:
            rows = pl.ds(c * CHUNK, CHUNK)
            c11[c] = [remote(u11.at[rows], v11r.at[rows], -1), remote(u11.at[rows], v11l.at[rows], 1)]

    arrived(c10a)
    run(10, [[(0, 512)], [(1536, 512)]])
    send11([0, 1, 6, 7])
    arrived(c10b)
    run(10, [[(768, 512)]])
    send11([3, 4])
    arrived(c10c)
    run(10, [[(512, 256), (1280, 256)]])
    send11([2, 5])

    weights(11)
    c12 = {}
    for c in ORDER:
        rows = pl.ds(c * CHUNK, CHUNK)
        arrived(c11[c])
        taps = jnp.where(has_l, v11l[rows, :], 0), jnp.where(has_r, v11r[rows, :], 0)
        tile = [(c * CHUNK, CHUNK)]
        finish(11, tile, pre_act(11, tile, taps))
        c12[c] = [remote(u12.at[rows], v12r.at[rows], -2), remote(u12.at[rows], v12l.at[rows], 2)]

    weights(12)
    c13 = {}
    for c in ORDER:
        rows = pl.ds(c * CHUNK, CHUNK)
        arrived(c12[c])
        taps = jnp.where(has_l2, v12l[rows, :], 0), jnp.where(has_r2, v12r[rows, :], 0)
        tile = [(c * CHUNK, CHUNK)]
        finish(12, tile, pre_act(12, tile, taps))
        c13[c] = [remote(u13.at[rows], v13.at[rows], None)]

    weights(13)
    out = []
    for c in ORDER:
        rows = pl.ds(c * CHUNK, CHUNK)
        arrived(c13[c])
        other = v13[rows, :]
        taps = jnp.where(low, 0, other), jnp.where(low, other, 0)
        tile = [(c * CHUNK, CHUNK)]
        finish(13, tile, pre_act(13, tile, taps))
        for j, cp in enumerate([pltpu.make_async_copy(ha.at[pl.ds(PAD + c * CHUNK, CHUNK)], h_ref.at[0, rows], osem.at[c, 0]),
                                pltpu.make_async_copy(sk.at[rows], s_ref.at[0, rows], osem.at[c, 1])]):
            cp.start()
            out.append(cp)

    for cp, dj in sent:
        if dj is None:
            cp.wait_send()
        else:
            @pl.when(have[dj])
            def _():
                cp.wait_send()
    for cp in out:
        cp.wait()


N_REMOTE = 2 + 2 + 4 + 6 + 16 + 16 + 8


def solution(mesh):
    act_spec = P('dp', 'sp', None)
    bf, f32 = jnp.bfloat16, jnp.float32

    def local_stack(x, w_in, w_res, w_skip):
        any_spec = pl.BlockSpec(memory_space=pl.ANY)
        u_big = [pltpu.VMEM((ROWS + 2 * EXT, CH), bf)] * 4
        return pl.pallas_call(
            kernel,
            out_shape=(jax.ShapeDtypeStruct(x.shape, f32), jax.ShapeDtypeStruct(x.shape, f32)),
            in_specs=[any_spec] * 4,
            out_specs=(any_spec, any_spec),
            scratch_shapes=[
                pltpu.VMEM((ROWS + 2 * EXT, CH), bf),
                pltpu.VMEM((ROWS + 2 * PAD, CH), f32), pltpu.VMEM((ROWS + 2 * PAD, CH), f32), pltpu.VMEM((ROWS, CH), f32),
                *u_big,
                pltpu.VMEM((ROWS + 512, CH), bf), pltpu.VMEM((ROWS + 1024, CH), bf), pltpu.VMEM((ROWS + 2048, CH), bf),
                *[pltpu.VMEM((ROWS, CH), bf)] * 8,
                pltpu.VMEM((14, 3 * CH, 2 * CH), bf), pltpu.VMEM((14, CH, 2 * CH), bf),
                pltpu.SemaphoreType.DMA, pltpu.SemaphoreType.DMA((14, 3)), pltpu.SemaphoreType.DMA((8, 2)),
                pltpu.SemaphoreType.DMA((N_REMOTE,)), pltpu.SemaphoreType.DMA((N_REMOTE,)),
            ],
            compiler_params=pltpu.CompilerParams(collective_id=0, has_side_effects=True, vmem_limit_bytes=56 * 1024 * 1024),
        )(x, w_in.reshape(14, 3 * CH, 2 * CH), w_res, w_skip)

    return jax.shard_map(local_stack, mesh=mesh, in_specs=(act_spec, P(), P(), P()), out_specs=(act_spec, act_spec), check_vma=False)
```

time: 171 us -> 74 us (0.43)
  starting transfers between devices: 93.6 us -> 0 us
  Pallas kernels: 0 us -> 69.9 us
  waiting for transfers between devices: 37 us -> 0 us
  matrix products: 28.1 us -> 0 us
  other arithmetic: 5.86 us -> 0 us
    ppermute x28 -> x0, starting transfers between devices: 93.6 us -> none  [the longest x11 50.9 us: neighbour_taps(): lax.ppermute(cur_bf[:, n_rows - dilation:], 'sp', [(src, src + 1) for src...]
    pallas_call x0 -> x1, Pallas kernels: none -> 69.9 us  [local_stack(): pl.pallas_call(kernel, out_shape=(jax.ShapeDtypeStruct(x.shape, f32), jax...]
    ppermute x28 -> x0, waiting for transfers between devices: 37 us -> none  [the longest x3 27.6 us: neighbour_taps(): lax.ppermute(cur_bf, 'sp', [(src + n_hops, src) for src in range(n_dev -...]
    dot_general x70 -> x0, matrix products: 28.1 us -> none  [the longest x14 6.63 us: local_stack(): jnp.einsum('bsc,cf->bsf', cur_bf, w_in[layer, 1], preferred_element_type=...]
    convert_element_type x14 -> x0, other arithmetic: 5.86 us -> none  [local_stack(): (jnp.tanh(pre_act[..., :n_chan]) * jax.nn.sigmoid(pre_act[..., n_chan:]))...]
    slice x21 -> x0, local copies, waits for them, and re-layouts: 3.19 us -> none  [the longest x10 2.33 us: neighbour_taps(): cur_bf[:, :n_rows - dilation]]
    unnamed x8 -> x4, local copies, waits for them, and re-layouts: 0.61 us -> 3.32 us
  transfers between devices with their start and end apart: 28 -> 0, of which waited for: 15 -> 0; matrix products, arithmetic and copies ran while one was open for 8% -> 0% of each run, Pallas kernels for 0% -> 0%
where the time goes in v1:
time: 74 us; the launch traced here: 73.9 us
  Pallas kernels  69.9 us (94%)
  local copies, waits for them, and re-layouts  3.32 us (4%)
    pallas_call x1, Pallas kernels, local_stack(): pl.pallas_call(kernel, out_shape=(jax.ShapeDtypeStruct(x.shape, f32), jax...  69.9 us
    unnamed x4, local copies, waits for them, and re-layouts  3.32 us

profile of v1, /device:TPU:0, one launch (start us, length us, event | category | flops | bytes accessed | tf_op | source)
XLA Modules:
  0.0 73.9 jit_solution(14494247765415572265)
XLA Ops:
  0.6 69.9 %shard_map.59 = (f32[1,2048,128]{2,1,0:T(8,128)}, f32[1,2048,128]{2,1,0:T(8,128)}) custom-call(bf16[1,2048,128]{2,1,0:T(8,128)(2,1)} %x_ref.1, bf16[14,384,256]{2,1,0:T(8,128)(2,1)} %bitcast.1, bf16[14,128,128]{2,1,0:T(8,128)(2,1)} %wres_ref.1, bf16[14,128,128]{2,1,0:T(8,128)(2,1)} %wskip_ref.1), custom_call_target="tpu_custom_call" | custom-call | tf_op jit(solution)/shard_map/pallas_call | solution.py:281
  70.5 0.0 copy-start
  70.6 2.4 %copy.8 = f32[1,2048,128]{2,1,0:T(8,128)} copy(f32[1,2048,128]{2,1,0:T(8,128)} %get-tuple-element.4) | data formatting | bytes 2097152
  72.9 0.0 copy-done
  72.9 1.0 %copy.9 = f32[1,2048,128]{2,1,0:T(8,128)} copy(f32[1,2048,128]{2,1,0:T(8,128)S(1)} %copy-done) | data formatting | bytes 2097152
Async XLA Ops:
  70.5 2.4 %copy-start = (f32[1,2048,128]{2,1,0:T(8,128)S(1)}, f32[1,2048,128]{2,1,0:T(8,128)}, u32[]{:S(2)}) copy-start(f32[1,2048,128]{2,1,0:T(8,128)} %get-tuple-element.5) | copy-start | bytes 3145732

commit v2 on v1

--- a/solution.py
+++ b/solution.py
@@ -15,11 +15,12 @@
 PAD = EXT + 16
 REACH = [256, 256, 256, 240, 224, 192, 128, 0]
 CHUNK = 256
+BARRIER_AFTER = 4
 ORDER = [0, 1, 6, 7, 3, 4, 2, 5]
 
 
 def kernel(x_ref, win_ref, wres_ref, wskip_ref, h_ref, s_ref,
-           xb, ha, hb, sk, u4, u5, u6, u7, u8, u9, u10, u11, u12, u13,
+           xb, h0, h1, h2, h3, ha, sk, u4, u5, u6, u7, u8, u9, u10, u11, u12, u13,
            v11l, v11r, v12l, v12r, v13, win, wrs, lsem, wsem, osem, ssem, rsem):
     me = lax.axis_index('sp')
     has_l, has_r = me >= 1, me <= N_DEV - 2
@@ -62,14 +63,7 @@
         zero(u8, 256 + ROWS, 256)
         zero(u9, 512 + ROWS, 512)
         zero(u10, 1024 + ROWS, 1024)
-    for buf in (ha, hb):
-        zero(buf, 0, 16)
-        zero(buf, PAD + ROWS + EXT, 16)
-
-    peers = 1
-    for ok in have.values():
-        peers += jnp.where(ok, 1, 0)
-    pl.semaphore_wait(barrier, peers)
+
 
     count = [0]
     sent = []
@@ -98,9 +92,6 @@
                 def _():
                     cp.wait_recv()
 
-    x_halo = [remote(x_ref.at[0, pl.ds(0, EXT)], xb.at[pl.ds(EXT + ROWS, EXT)], -1),
-              remote(x_ref.at[0, pl.ds(ROWS - EXT, EXT)], xb.at[pl.ds(0, EXT)], 1)]
-
     u_ref = {4: (u4, EXT), 5: (u5, EXT), 6: (u6, EXT), 7: (u7, EXT), 8: (u8, 256), 9: (u9, 512), 10: (u10, 1024),
              11: (u11, 0), 12: (u12, 0), 13: (u13, 0)}
 
@@ -109,9 +100,7 @@
         return parts[0] if len(parts) == 1 else jnp.concatenate(parts, axis=0)
 
     def state(k):
-        if k < 4:
-            return ((ha, hb), (hb, ha))[k % 2]
-        return ha, ha
+        return (h0, h1, h2, h3, ha)[min(k, 4)], (h0, h1, h2, h3, ha)[min(k + 1, 4)]
 
     def pre_act(k, tile, taps=None):
         d = 2 ** k
@@ -169,13 +158,28 @@
             c.wait()
 
     own_x.wait()
+    h0[pl.ds(PAD, ROWS), :] = xb[pl.ds(EXT, ROWS), :].astype(jnp.float32)
+    inner = [[(i * 512, 512)] for i in range(4)]
+    for k in range(BARRIER_AFTER):
+        weights(k)
+        run(k, inner)
+    peers = 1
+    for ok in have.values():
+        peers += jnp.where(ok, 1, 0)
+    pl.semaphore_wait(barrier, peers)
+    x_halo = [remote(x_ref.at[0, pl.ds(0, EXT)], xb.at[pl.ds(EXT + ROWS, EXT)], -1),
+              remote(x_ref.at[0, pl.ds(ROWS - EXT, EXT)], xb.at[pl.ds(0, EXT)], 1)]
+
+    for k in range(BARRIER_AFTER, 7):
+        weights(k)
+        run(k, inner)
+
     arrived(x_halo)
-    ha[pl.ds(16, ROWS + 2 * EXT), :] = xb[...].astype(jnp.float32)
-
+    h0[pl.ds(16, EXT), :] = xb[pl.ds(0, EXT), :].astype(jnp.float32)
+    h0[pl.ds(PAD + ROWS, EXT), :] = xb[pl.ds(EXT + ROWS, EXT), :].astype(jnp.float32)
     for k in range(7):
-        weights(k)
         e = REACH[k]
-        run(k, [[(-e, 256 + e)], [(256, 512)], [(768, 512)], [(1280, 512)], [(1792, 256 + e)]])
+        run(k, [[(-e, 128 + e)], [(ROWS - 128, 128 + e)]])
     weights(7)
     run(7, [[(0, 256), (1792, 256)]])
     c8 = [remote(u8.at[pl.ds(256, 256)], u8.at[pl.ds(256 + ROWS, 256)], -1),
@@ -285,7 +289,7 @@
             out_specs=(any_spec, any_spec),
             scratch_shapes=[
                 pltpu.VMEM((ROWS + 2 * EXT, CH), bf),
-                pltpu.VMEM((ROWS + 2 * PAD, CH), f32), pltpu.VMEM((ROWS + 2 * PAD, CH), f32), pltpu.VMEM((ROWS, CH), f32),
+                *[pltpu.VMEM((ROWS + 2 * PAD, CH), f32)] * 5, pltpu.VMEM((ROWS, CH), f32),
                 *u_big,
                 pltpu.VMEM((ROWS + 512, CH), bf), pltpu.VMEM((ROWS + 1024, CH), bf), pltpu.VMEM((ROWS + 2048, CH), bf),
                 *[pltpu.VMEM((ROWS, CH), bf)] * 8,

time: 74 us -> 73.2 us (0.989)
  Pallas kernels: 69.9 us -> 69.1 us
    pallas_call x1, Pallas kernels: 69.9 us -> 69.1 us  [local_stack(): pl.pallas_call(kernel, out_shape=(jax.ShapeDtypeStruct(x.shape, f32), jax...]
where the time goes in v2:
time: 73.2 us; the launch traced here: 73 us
  Pallas kernels  69.1 us (94%)
  local copies, waits for them, and re-layouts  3.32 us (5%)
    pallas_call x1, Pallas kernels, local_stack(): pl.pallas_call(kernel, out_shape=(jax.ShapeDtypeStruct(x.shape, f32), jax...  69.1 us
    unnamed x4, local copies, waits for them, and re-layouts  3.32 us

profile of v2, /device:TPU:0, one launch (start us, length us, event | category | flops | bytes accessed | tf_op | source)
XLA Modules:
  0.0 73.0 jit_solution(1877552945501936755)
XLA Ops:
  0.6 69.1 %shard_map.59 = (f32[1,2048,128]{2,1,0:T(8,128)}, f32[1,2048,128]{2,1,0:T(8,128)}) custom-call(bf16[1,2048,128]{2,1,0:T(8,128)(2,1)} %x_ref.1, bf16[14,384,256]{2,1,0:T(8,128)(2,1)} %bitcast.1, bf16[14,128,128]{2,1,0:T(8,128)(2,1)} %wres_ref.1, bf16[14,128,128]{2,1,0:T(8,128)(2,1)} %wskip_ref.1), custom_call_target="tpu_custom_call" | custom-call | tf_op jit(solution)/shard_map/pallas_call | solution.py:285
  69.7 0.0 copy-start
  69.7 2.4 %copy.8 = f32[1,2048,128]{2,1,0:T(8,128)} copy(f32[1,2048,128]{2,1,0:T(8,128)} %get-tuple-element.4) | data formatting | bytes 2097152
  72.1 0.0 copy-done
  72.1 1.0 %copy.9 = f32[1,2048,128]{2,1,0:T(8,128)} copy(f32[1,2048,128]{2,1,0:T(8,128)S(1)} %copy-done) | data formatting | bytes 2097152
Async XLA Ops:
  69.7 2.4 %copy-start = (f32[1,2048,128]{2,1,0:T(8,128)S(1)}, f32[1,2048,128]{2,1,0:T(8,128)}, u32[]{:S(2)}) copy-start(f32[1,2048,128]{2,1,0:T(8,128)} %get-tuple-element.5) | copy-start | bytes 3145732

commit v3 on v2

--- a/solution.py
+++ b/solution.py
@@ -15,19 +15,27 @@
 PAD = EXT + 16
 REACH = [256, 256, 256, 240, 224, 192, 128, 0]
 CHUNK = 256
-BARRIER_AFTER = 4
-ORDER = [0, 1, 6, 7, 3, 4, 2, 5]
+BARRIER_AFTER = 2
+ORDER = [1, 6, 0, 7, 3, 4, 2, 5]
 
 
 def kernel(x_ref, win_ref, wres_ref, wskip_ref, h_ref, s_ref,
            xb, h0, h1, h2, h3, ha, sk, u4, u5, u6, u7, u8, u9, u10, u11, u12, u13,
-           v11l, v11r, v12l, v12r, v13, win, wrs, lsem, wsem, osem, ssem, rsem):
+           v11, v12l, v12r, v13, win, wrs, lsem, wsem, osem, ssem, rsem, s11, r11):
     me = lax.axis_index('sp')
     has_l, has_r = me >= 1, me <= N_DEV - 2
     has_l2, has_r2 = me >= 2, me <= N_DEV - 3
     low = me < N_DEV // 2
     partner = jnp.where(low, me + N_DEV // 2, me - N_DEV // 2)
-    have = {-1: has_l, 1: has_r, -2: has_l2, 2: has_r2}
+    even = lax.rem(me, 2) == 0
+    has_o = (me >= 1) & (me <= N_DEV - 2)
+    inner, outer = jnp.where(even, me + 1, me - 1), jnp.where(even, me - 1, me + 1)
+    have = {-1: has_l, 1: has_r, -2: has_l2, 2: has_r2, 'outer': has_o, 'inner': None, 'partner': None}
+    device = {-2: me - 2, 2: me + 2, 'outer': outer, 'inner': inner, 'partner': partner}
+    across = {'inner': jnp.where(even, -ROWS, ROWS), 'outer': jnp.where(even, ROWS, -ROWS)}
+
+    def from_inner(p, n):
+        return pl.multiple_of(jnp.where(even, ROWS - p - n, p), 256)
 
     loads = []
     own_x = pltpu.make_async_copy(x_ref.at[0], xb.at[pl.ds(EXT, ROWS)], lsem)
@@ -41,8 +49,8 @@
         loads.append(trio)
 
     barrier = pltpu.get_barrier_semaphore()
-    for dj, ok in have.items():
-        @pl.when(ok)
+    for dj in (-2, -1, 1, 2):
+        @pl.when(have[dj])
         def _():
             pl.semaphore_signal(barrier, inc=1, device_id={'sp': me + dj}, device_id_type=MESH)
     pl.semaphore_signal(barrier, inc=1, device_id={'sp': partner}, device_id_type=MESH)
@@ -68,29 +76,36 @@
     count = [0]
     sent = []
 
-    def remote(src, dst, dj):
+    def start(cp, to):
+        if have[to] is None:
+            cp.start()
+        else:
+            @pl.when(have[to])
+            def _():
+                cp.start()
+
+    def remote(src, dst, to):
         i = count[0]
         count[0] += 1
-        dev = partner if dj is None else me + dj
         cp = pltpu.make_async_remote_copy(src_ref=src, dst_ref=dst, send_sem=ssem.at[i], recv_sem=rsem.at[i],
-                                          device_id={'sp': dev}, device_id_type=MESH)
-        if dj is None:
-            cp.start()
-        else:
-            @pl.when(have[dj])
-            def _():
-                cp.start()
-        sent.append((cp, dj))
-        return cp, dj
+                                          device_id={'sp': device[to]}, device_id_type=MESH)
+        start(cp, to)
+        sent.append((cp, to))
+        return cp, to
 
     def arrived(copies):
-        for cp, dj in copies:
-            if dj is None:
+        for cp, to in copies:
+            came = have[-to] if isinstance(to, int) else have[to]
+            if came is None:
                 cp.wait_recv()
             else:
-                @pl.when(have[-dj])
+                @pl.when(came)
                 def _():
                     cp.wait_recv()
+
+    def halo(ref, base, to, p, n):
+        row = base + from_inner(p, n)
+        return remote(ref.at[pl.ds(row, n)], ref.at[pl.ds(row + across[to], n)], to)
 
     u_ref = {4: (u4, EXT), 5: (u5, EXT), 6: (u6, EXT), 7: (u7, EXT), 8: (u8, 256), 9: (u9, 512), 10: (u10, 1024),
              11: (u11, 0), 12: (u12, 0), 13: (u13, 0)}
@@ -121,7 +136,7 @@
         pieces, off = [], 0
         for r, n in tile:
             g = gate[off:off + n]
-            before, after = max(0, -r), max(0, r + n - ROWS)
+            before, after = (max(0, -r), max(0, r + n - ROWS)) if isinstance(r, int) else (0, 0)
             if before:
                 g = jnp.concatenate([jnp.where(has_l, g[:before], 0.0), g[before:]], axis=0)
             if after:
@@ -138,12 +153,12 @@
             if 4 <= k + 1 <= 13:
                 ref, base = u_ref[k + 1]
                 ref[pl.ds(base + r, n), :] = new.astype(jnp.bfloat16)
-            lo, hi = max(r, 0), min(r + n, ROWS)
-            part = y[off + lo - r:off + hi - r, CH:]
+            lo, m = r + before, n - before - after
+            part = y[off + before:off + before + m, CH:]
             if k == 0:
-                sk[pl.ds(lo, hi - lo), :] = part
+                sk[pl.ds(lo, m), :] = part
             else:
-                sk[pl.ds(lo, hi - lo), :] += part
+                sk[pl.ds(lo, m), :] += part
             off += n
 
     def run(k, tiles):
@@ -164,12 +179,10 @@
         weights(k)
         run(k, inner)
     peers = 1
-    for ok in have.values():
-        peers += jnp.where(ok, 1, 0)
+    for dj in (-2, -1, 1, 2):
+        peers += jnp.where(have[dj], 1, 0)
     pl.semaphore_wait(barrier, peers)
-    x_halo = [remote(x_ref.at[0, pl.ds(0, EXT)], xb.at[pl.ds(EXT + ROWS, EXT)], -1),
-              remote(x_ref.at[0, pl.ds(ROWS - EXT, EXT)], xb.at[pl.ds(0, EXT)], 1)]
-
+    x_halo = [halo(xb, EXT, 'outer', ROWS - EXT, EXT), halo(xb, EXT, 'inner', 0, EXT)]
     for k in range(BARRIER_AFTER, 7):
         weights(k)
         run(k, inner)
@@ -180,59 +193,79 @@
     for k in range(7):
         e = REACH[k]
         run(k, [[(-e, 128 + e)], [(ROWS - 128, 128 + e)]])
+    def side(p, n):
+        return [(from_inner(p, n), n)]
+
     weights(7)
     run(7, [[(0, 256), (1792, 256)]])
-    c8 = [remote(u8.at[pl.ds(256, 256)], u8.at[pl.ds(256 + ROWS, 256)], -1),
-          remote(u8.at[pl.ds(ROWS, 256)], u8.at[pl.ds(0, 256)], 1)]
+    o8 = halo(u8, 256, 'outer', 1792, 256)
+    i8 = halo(u8, 256, 'inner', 0, 256)
     run(7, [[(256, 512)], [(768, 512)], [(1280, 512)]])
 
-    def edge9(r):
-        return remote(u9.at[pl.ds(512 + r, 256)], u9.at[pl.ds(512 + r + (ROWS if r < 512 else -ROWS), 256)], -1 if r < 512 else 1)
-
     weights(8)
-    run(8, [[(256, 512)], [(768, 512)], [(1280, 512)]])
-    c9a = [edge9(256), edge9(1536)]
-    arrived(c8)
-    run(8, [[(0, 256), (1792, 256)]])
-    c9b = [edge9(0), edge9(1792)]
-
-    def edge10(r, n):
-        return remote(u10.at[pl.ds(1024 + r, n)], u10.at[pl.ds(1024 + r + (ROWS if r < 1024 else -ROWS), n)], -1 if r < 1024 else 1)
+    arrived([i8])
+    run(8, [side(0, 256), [(256, 512)], [(768, 512)], [(1280, 512)]])
+    o9a = halo(u9, 512, 'outer', 1536, 256)
+    i9 = halo(u9, 512, 'inner', 0, 512)
+    arrived([o8])
+    run(8, [side(1792, 256)])
+    o9b = halo(u9, 512, 'outer', 1792, 256)
 
     weights(9)
     run(9, [[(512, 512)], [(1024, 512)]])
-    c10a = [edge10(512, 512), edge10(1024, 512)]
-    arrived(c9a)
-    run(9, [[(0, 256), (1792, 256)]])
-    c10b = [edge10(0, 256), edge10(1792, 256)]
-    arrived(c9b)
-    run(9, [[(256, 256), (1536, 256)]])
-    c10c = [edge10(256, 256), edge10(1536, 256)]
+    o10a = halo(u10, 1024, 'outer', 1024, 512)
+    i10a = halo(u10, 1024, 'inner', 512, 512)
+    arrived([i9])
+    run(9, [side(0, 512)])
+    i10b = halo(u10, 1024, 'inner', 0, 512)
+    arrived([o9a])
+    run(9, [side(1792, 256)])
+    o10b = halo(u10, 1024, 'outer', 1792, 256)
+    arrived([o9b])
+    run(9, [side(1536, 256)])
+    o10c = halo(u10, 1024, 'outer', 1536, 256)
 
     weights(10)
+
+    def copies11(c, rows):
+        made = []
+        for lane, to in enumerate(('outer', 'inner')):
+            slot = jnp.where(even, 1 - lane, lane)
+            made.append((pltpu.make_async_remote_copy(
+                src_ref=u11.at[rows], dst_ref=v11.at[slot, rows], send_sem=s11.at[c, lane], recv_sem=r11.at[c, lane],
+                device_id={'sp': device[to]}, device_id_type=MESH), to))
+        return made
+
+    def send11(p, n):
+        for q in range(p, p + n, CHUNK):
+            row = from_inner(q, CHUNK)
+            for cp, to in copies11(row // CHUNK, pl.ds(row, CHUNK)):
+                start(cp, to)
+
+    arrived([i10a])
+    run(10, [side(0, 512)])
+    send11(0, 512)
+    arrived([i10b])
+    run(10, [side(512, 512)])
+    send11(512, 512)
+    arrived([o10a])
+    run(10, [side(1536, 512)])
+    send11(1536, 512)
+    arrived([o10b])
+    run(10, [side(1024, 256)])
+    send11(1024, 256)
+    arrived([o10c])
+    run(10, [side(1280, 256)])
+    send11(1280, 256)
+
+    weights(11)
     c11 = {}
-
-    def send11(chunks):
-        for c in chunks:
-            rows = pl.ds(c * CHUNK, CHUNK)
-            c11[c] = [remote(u11.at[rows], v11r.at[rows], -1), remote(u11.at[rows], v11l.at[rows], 1)]
-
-    arrived(c10a)
-    run(10, [[(0, 512)], [(1536, 512)]])
-    send11([0, 1, 6, 7])
-    arrived(c10b)
-    run(10, [[(768, 512)]])
-    send11([3, 4])
-    arrived(c10c)
-    run(10, [[(512, 256), (1280, 256)]])
-    send11([2, 5])
-
-    weights(11)
     c12 = {}
     for c in ORDER:
         rows = pl.ds(c * CHUNK, CHUNK)
+        c11[c] = copies11(c, rows)
         arrived(c11[c])
-        taps = jnp.where(has_l, v11l[rows, :], 0), jnp.where(has_r, v11r[rows, :], 0)
+        taps = jnp.where(has_l, v11[0, rows, :], 0), jnp.where(has_r, v11[1, rows, :], 0)
         tile = [(c * CHUNK, CHUNK)]
         finish(11, tile, pre_act(11, tile, taps))
         c12[c] = [remote(u12.at[rows], v12r.at[rows], -2), remote(u12.at[rows], v12l.at[rows], 2)]
@@ -245,7 +278,7 @@
         taps = jnp.where(has_l2, v12l[rows, :], 0), jnp.where(has_r2, v12r[rows, :], 0)
         tile = [(c * CHUNK, CHUNK)]
         finish(12, tile, pre_act(12, tile, taps))
-        c13[c] = [remote(u13.at[rows], v13.at[rows], None)]
+        c13[c] = [remote(u13.at[rows], v13.at[rows], 'partner')]
 
     weights(13)
     out = []
@@ -261,18 +294,18 @@
             cp.start()
             out.append(cp)
 
-    for cp, dj in sent:
-        if dj is None:
+    for cp, to in sent + [pair for made in c11.values() for pair in made]:
+        if have[to] is None:
             cp.wait_send()
         else:
-            @pl.when(have[dj])
+            @pl.when(have[to])
             def _():
                 cp.wait_send()
     for cp in out:
         cp.wait()
 
 
-N_REMOTE = 2 + 2 + 4 + 6 + 16 + 16 + 8
+N_REMOTE = 2 + 2 + 3 + 5 + 16 + 8
 
 
 def solution(mesh):
@@ -292,10 +325,11 @@
                 *[pltpu.VMEM((ROWS + 2 * PAD, CH), f32)] * 5, pltpu.VMEM((ROWS, CH), f32),
                 *u_big,
                 pltpu.VMEM((ROWS + 512, CH), bf), pltpu.VMEM((ROWS + 1024, CH), bf), pltpu.VMEM((ROWS + 2048, CH), bf),
-                *[pltpu.VMEM((ROWS, CH), bf)] * 8,
+                *[pltpu.VMEM((ROWS, CH), bf)] * 3, pltpu.VMEM((2, ROWS, CH), bf), *[pltpu.VMEM((ROWS, CH), bf)] * 3,
                 pltpu.VMEM((14, 3 * CH, 2 * CH), bf), pltpu.VMEM((14, CH, 2 * CH), bf),
                 pltpu.SemaphoreType.DMA, pltpu.SemaphoreType.DMA((14, 3)), pltpu.SemaphoreType.DMA((8, 2)),
                 pltpu.SemaphoreType.DMA((N_REMOTE,)), pltpu.SemaphoreType.DMA((N_REMOTE,)),
+                pltpu.SemaphoreType.DMA((8, 2)), pltpu.SemaphoreType.DMA((8, 2)),
             ],
             compiler_params=pltpu.CompilerParams(collective_id=0, has_side_effects=True, vmem_limit_bytes=56 * 1024 * 1024),
         )(x, w_in.reshape(14, 3 * CH, 2 * CH), w_res, w_skip)

time: 73.2 us -> 71.2 us (0.973)
  the two profiles are of different devices: /device:TPU:0 before, /device:TPU:1 now
where the time goes in v3:
time: 71.2 us; the launch traced here: 71 us
  Pallas kernels  67 us (94%)
  local copies, waits for them, and re-layouts  3.32 us (5%)
    pallas_call x1, Pallas kernels, local_stack(): pl.pallas_call(kernel, out_shape=(jax.ShapeDtypeStruct(x.shape, f32), jax...  67 us
    unnamed x4, local copies, waits for them, and re-layouts  3.32 us

profile of v3, /device:TPU:1, one launch (start us, length us, event | category | flops | bytes accessed | tf_op | source)
XLA Modules:
  0.0 71.0 jit_solution(6509400701975265645)
XLA Ops:
  0.6 67.0 %shard_map.59 = (f32[1,2048,128]{2,1,0:T(8,128)}, f32[1,2048,128]{2,1,0:T(8,128)}) custom-call(bf16[1,2048,128]{2,1,0:T(8,128)(2,1)} %x_ref.1, bf16[14,384,256]{2,1,0:T(8,128)(2,1)} %bitcast.1, bf16[14,128,128]{2,1,0:T(8,128)(2,1)} %wres_ref.1, bf16[14,128,128]{2,1,0:T(8,128)(2,1)} %wskip_ref.1), custom_call_target="tpu_custom_call" | custom-call | tf_op jit(solution)/shard_map/pallas_call | solution.py:318
  67.7 0.0 copy-start
  67.7 2.4 %copy.8 = f32[1,2048,128]{2,1,0:T(8,128)} copy(f32[1,2048,128]{2,1,0:T(8,128)} %get-tuple-element.4) | data formatting | bytes 2097152
  70.0 0.0 copy-done
  70.0 1.0 %copy.9 = f32[1,2048,128]{2,1,0:T(8,128)} copy(f32[1,2048,128]{2,1,0:T(8,128)S(1)} %copy-done) | data formatting | bytes 2097152
Async XLA Ops:
  67.7 2.4 %copy-start = (f32[1,2048,128]{2,1,0:T(8,128)S(1)}, f32[1,2048,128]{2,1,0:T(8,128)}, u32[]{:S(2)}) copy-start(f32[1,2048,128]{2,1,0:T(8,128)} %get-tuple-element.5) | copy-start | bytes 3145732

commit v4 on v3

--- a/solution.py
+++ b/solution.py
@@ -15,7 +15,7 @@
 PAD = EXT + 16
 REACH = [256, 256, 256, 240, 224, 192, 128, 0]
 CHUNK = 256
-BARRIER_AFTER = 2
+BAND = [496, 512, 512, 496, 480, 448, 384, 256]
 ORDER = [1, 6, 0, 7, 3, 4, 2, 5]
 
 
@@ -103,9 +103,16 @@
                 def _():
                     cp.wait_recv()
 
-    def halo(ref, base, to, p, n):
-        row = base + from_inner(p, n)
-        return remote(ref.at[pl.ds(row, n)], ref.at[pl.ds(row + across[to], n)], to)
+    def halo(ref, base, to, p, n, source=None):
+        row = from_inner(p, n)
+        src = ref.at[pl.ds(base + row, n)] if source is None else source.at[0, pl.ds(row, n)]
+        return remote(src, ref.at[pl.ds(base + row + across[to], n)], to)
+
+    peers = 1
+    for dj in (-2, -1, 1, 2):
+        peers += jnp.where(have[dj], 1, 0)
+    pl.semaphore_wait(barrier, peers)
+    x_halo = [halo(xb, EXT, 'outer', ROWS - EXT, EXT, x_ref), halo(xb, EXT, 'inner', 0, EXT, x_ref)]
 
     u_ref = {4: (u4, EXT), 5: (u5, EXT), 6: (u6, EXT), 7: (u7, EXT), 8: (u8, 256), 9: (u9, 512), 10: (u10, 1024),
              11: (u11, 0), 12: (u12, 0), 13: (u13, 0)}
@@ -161,68 +168,88 @@
                 sk[pl.ds(lo, m), :] += part
             off += n
 
-    def run(k, tiles):
-        z = {i: pre_act(k, tiles[i]) for i in range(min(2, len(tiles)))}
-        for i in range(len(tiles)):
-            if i + 2 < len(tiles):
-                z[i + 2] = pre_act(k, tiles[i + 2])
-            finish(k, tiles[i], z.pop(i))
+    waited = set()
 
     def weights(k):
-        for c in loads[k]:
-            c.wait()
+        if k not in waited:
+            waited.add(k)
+            for c in loads[k]:
+                c.wait()
+
+    def reads(task, earlier):
+        (k, tile), (k0, tile0) = task, earlier
+        if k0 != k - 1:
+            return False
+        d = 2 ** k
+        for r, n in tile:
+            for r0, n0 in tile0:
+                if not isinstance(r, int) or not isinstance(r0, int):
+                    return True
+                if any(r + o < r0 + n0 and r0 < r + o + n for o in (-d, 0, d)):
+                    return True
+        return False
+
+    def run(tasks):
+        pending = []
+
+        def retire(count):
+            for _ in range(count):
+                k, tile, z = pending.pop(0)
+                finish(k, tile, z)
+        for task in tasks:
+            weights(task[0])
+            needed = [i for i, p in enumerate(pending) if reads(task, p[:2])]
+            if needed:
+                retire(needed[-1] + 1)
+            z = pre_act(*task)
+            if len(pending) == 2:
+                retire(1)
+            pending.append((*task, z))
+        retire(len(pending))
+
+    def split(lo, hi, count):
+        cuts = [lo + (hi - lo) * i // count // 16 * 16 for i in range(count)] + [hi]
+        return [[(p, q - p)] for p, q in zip(cuts, cuts[1:])]
+
+    def interior(k):
+        return [(k, t) for t in split(BAND[k], ROWS - BAND[k], 4 if k == 7 else 3 if k == 6 else 2)]
+
+    def bands(k):
+        e, b = REACH[k], BAND[k]
+        n = 2 if k < 7 else 1
+        return [(k, t) for t in split(-e, b, n) + split(ROWS - b, ROWS + e, n)]
 
     own_x.wait()
     h0[pl.ds(PAD, ROWS), :] = xb[pl.ds(EXT, ROWS), :].astype(jnp.float32)
-    inner = [[(i * 512, 512)] for i in range(4)]
-    for k in range(BARRIER_AFTER):
-        weights(k)
-        run(k, inner)
-    peers = 1
-    for dj in (-2, -1, 1, 2):
-        peers += jnp.where(have[dj], 1, 0)
-    pl.semaphore_wait(barrier, peers)
-    x_halo = [halo(xb, EXT, 'outer', ROWS - EXT, EXT), halo(xb, EXT, 'inner', 0, EXT)]
-    for k in range(BARRIER_AFTER, 7):
-        weights(k)
-        run(k, inner)
-
+    run(interior(0) + interior(1))
     arrived(x_halo)
     h0[pl.ds(16, EXT), :] = xb[pl.ds(0, EXT), :].astype(jnp.float32)
     h0[pl.ds(PAD + ROWS, EXT), :] = xb[pl.ds(EXT + ROWS, EXT), :].astype(jnp.float32)
-    for k in range(7):
-        e = REACH[k]
-        run(k, [[(-e, 128 + e)], [(ROWS - 128, 128 + e)]])
+    run([task for k in range(8) for task in bands(k)])
+
     def side(p, n):
         return [(from_inner(p, n), n)]
 
-    weights(7)
-    run(7, [[(0, 256), (1792, 256)]])
     o8 = halo(u8, 256, 'outer', 1792, 256)
     i8 = halo(u8, 256, 'inner', 0, 256)
-    run(7, [[(256, 512)], [(768, 512)], [(1280, 512)]])
-
-    weights(8)
-    arrived([i8])
-    run(8, [side(0, 256), [(256, 512)], [(768, 512)], [(1280, 512)]])
+    run([task for k in range(2, 8) for task in interior(k)])
+
+    arrived([i8, o8])
+    run([(8, side(1536, 512)), (8, side(0, 512))])
     o9a = halo(u9, 512, 'outer', 1536, 256)
+    o9b = halo(u9, 512, 'outer', 1792, 256)
     i9 = halo(u9, 512, 'inner', 0, 512)
-    arrived([o8])
-    run(8, [side(1792, 256)])
-    o9b = halo(u9, 512, 'outer', 1792, 256)
-
-    weights(9)
-    run(9, [[(512, 512)], [(1024, 512)]])
+    run([(8, [(512, 512)]), (8, [(1024, 512)]), (9, [(512, 512)]), (9, [(1024, 512)])])
     o10a = halo(u10, 1024, 'outer', 1024, 512)
     i10a = halo(u10, 1024, 'inner', 512, 512)
     arrived([i9])
-    run(9, [side(0, 512)])
+    run([(9, side(0, 512))])
     i10b = halo(u10, 1024, 'inner', 0, 512)
     arrived([o9a])
-    run(9, [side(1792, 256)])
+    run([(9, side(1792, 256))])
     o10b = halo(u10, 1024, 'outer', 1792, 256)
     arrived([o9b])
-    run(9, [side(1536, 256)])
+    run([(9, side(1536, 256))])
     o10c = halo(u10, 1024, 'outer', 1536, 256)
 
     weights(10)
@@ -243,19 +270,19 @@
                 start(cp, to)
 
     arrived([i10a])
-    run(10, [side(0, 512)])
+    run([(10, side(0, 512))])
     send11(0, 512)
     arrived([i10b])
-    run(10, [side(512, 512)])
+    run([(10, side(512, 512))])
     send11(512, 512)
     arrived([o10a])
-    run(10, [side(1536, 512)])
+    run([(10, side(1536, 512))])
     send11(1536, 512)
     arrived([o10b])
-    run(10, [side(1024, 256)])
+    run([(10, side(1024, 256))])
     send11(1024, 256)
     arrived([o10c])
-    run(10, [side(1280, 256)])
+    run([(10, side(1280, 256))])
     send11(1280, 256)
 
     weights(11)

time: 71.2 us -> 70 us (0.983)
  Pallas kernels: 67 us -> 65.9 us
    pallas_call x1, Pallas kernels: 67 us -> 65.9 us  [local_stack(): pl.pallas_call(kernel, out_shape=(jax.ShapeDtypeStruct(x.shape, f32), jax...]
where the time goes in v4:
time: 70 us; the launch traced here: 69.9 us
  Pallas kernels  65.9 us (94%)
  local copies, waits for them, and re-layouts  3.32 us (5%)
    pallas_call x1, Pallas kernels, local_stack(): pl.pallas_call(kernel, out_shape=(jax.ShapeDtypeStruct(x.shape, f32), jax...  65.9 us
    unnamed x4, local copies, waits for them, and re-layouts  3.32 us

profile of v4, /device:TPU:1, one launch (start us, length us, event | category | flops | bytes accessed | tf_op | source)
XLA Modules:
  0.0 69.9 jit_solution(862612721680223606)
XLA Ops:
  0.6 65.9 %shard_map.59 = (f32[1,2048,128]{2,1,0:T(8,128)}, f32[1,2048,128]{2,1,0:T(8,128)}) custom-call(bf16[1,2048,128]{2,1,0:T(8,128)(2,1)} %x_ref.1, bf16[14,384,256]{2,1,0:T(8,128)(2,1)} %bitcast.1, bf16[14,128,128]{2,1,0:T(8,128)(2,1)} %wres_ref.1, bf16[14,128,128]{2,1,0:T(8,128)(2,1)} %wskip_ref.1), custom_call_target="tpu_custom_call" | custom-call | tf_op jit(solution)/shard_map/pallas_call | solution.py:345
  66.5 0.0 copy-start
  66.6 2.4 %copy.8 = f32[1,2048,128]{2,1,0:T(8,128)} copy(f32[1,2048,128]{2,1,0:T(8,128)} %get-tuple-element.4) | data formatting | bytes 2097152
  68.9 0.0 copy-done
  68.9 1.0 %copy.9 = f32[1,2048,128]{2,1,0:T(8,128)} copy(f32[1,2048,128]{2,1,0:T(8,128)S(1)} %copy-done) | data formatting | bytes 2097152
Async XLA Ops:
  66.5 2.4 %copy-start = (f32[1,2048,128]{2,1,0:T(8,128)S(1)}, f32[1,2048,128]{2,1,0:T(8,128)}, u32[]{:S(2)}) copy-start(f32[1,2048,128]{2,1,0:T(8,128)} %get-tuple-element.5) | copy-start | bytes 3145732

commit v5 on v4

--- a/solution.py
+++ b/solution.py
@@ -15,13 +15,15 @@
 PAD = EXT + 16
 REACH = [256, 256, 256, 240, 224, 192, 128, 0]
 CHUNK = 256
+AHEAD = 3
 BAND = [496, 512, 512, 496, 480, 448, 384, 256]
+EARLY = 2
 ORDER = [1, 6, 0, 7, 3, 4, 2, 5]
 
 
-def kernel(x_ref, win_ref, wres_ref, wskip_ref, h_ref, s_ref,
+def kernel(x_ref, win_ref, wres_ref, wskip_ref, h_ref, s_ref, v13,
            xb, h0, h1, h2, h3, ha, sk, u4, u5, u6, u7, u8, u9, u10, u11, u12, u13,
-           v11, v12l, v12r, v13, win, wrs, lsem, wsem, osem, ssem, rsem, s11, r11):
+           v11, v12l, v12r, win, wrs, lsem, wsem, osem, ssem, rsem, s11, r11):
     me = lax.axis_index('sp')
     has_l, has_r = me >= 1, me <= N_DEV - 2
     has_l2, has_r2 = me >= 2, me <= N_DEV - 3
@@ -40,7 +42,7 @@
     loads = []
     own_x = pltpu.make_async_copy(x_ref.at[0], xb.at[pl.ds(EXT, ROWS)], lsem)
     own_x.start()
-    for k in range(14):
+    for k in range(13):
         trio = [pltpu.make_async_copy(win_ref.at[k], win.at[k], wsem.at[k, 0]),
                 pltpu.make_async_copy(wres_ref.at[k], wrs.at[k, :, pl.ds(0, CH)], wsem.at[k, 1]),
                 pltpu.make_async_copy(wskip_ref.at[k], wrs.at[k, :, pl.ds(CH, CH)], wsem.at[k, 2])]
@@ -49,11 +51,10 @@
         loads.append(trio)
 
     barrier = pltpu.get_barrier_semaphore()
-    for dj in (-2, -1, 1, 2):
+    for dj in (-1, 1):
         @pl.when(have[dj])
         def _():
             pl.semaphore_signal(barrier, inc=1, device_id={'sp': me + dj}, device_id_type=MESH)
-    pl.semaphore_signal(barrier, inc=1, device_id={'sp': partner}, device_id_type=MESH)
 
     def zero(ref, start, count):
         ref[pl.ds(start, count), :] = jnp.zeros((count, CH), ref.dtype)
@@ -84,12 +85,13 @@
             def _():
                 cp.start()
 
-    def remote(src, dst, to):
+    def remote(src, dst, to, now=True):
         i = count[0]
         count[0] += 1
         cp = pltpu.make_async_remote_copy(src_ref=src, dst_ref=dst, send_sem=ssem.at[i], recv_sem=rsem.at[i],
                                           device_id={'sp': device[to]}, device_id_type=MESH)
-        start(cp, to)
+        if now:
+            start(cp, to)
         sent.append((cp, to))
         return cp, to
 
@@ -108,10 +110,7 @@
         src = ref.at[pl.ds(base + row, n)] if source is None else source.at[0, pl.ds(row, n)]
         return remote(src, ref.at[pl.ds(base + row + across[to], n)], to)
 
-    peers = 1
-    for dj in (-2, -1, 1, 2):
-        peers += jnp.where(have[dj], 1, 0)
-    pl.semaphore_wait(barrier, peers)
+    pl.semaphore_wait(barrier, jnp.where(has_o, 2, 1))
     x_halo = [halo(xb, EXT, 'outer', ROWS - EXT, EXT, x_ref), halo(xb, EXT, 'inner', 0, EXT, x_ref)]
 
     u_ref = {4: (u4, EXT), 5: (u5, EXT), 6: (u6, EXT), 7: (u7, EXT), 8: (u8, 256), 9: (u9, 512), 10: (u10, 1024),
@@ -212,16 +211,31 @@
         return [[(p, q - p)] for p, q in zip(cuts, cuts[1:])]
 
     def interior(k):
-        return [(k, t) for t in split(BAND[k], ROWS - BAND[k], 4 if k == 7 else 3 if k == 6 else 2)]
+        return [(k, t) for t in split(BAND[k], ROWS - BAND[k], 3 if k >= 6 else 2)]
 
     def bands(k):
         e, b = REACH[k], BAND[k]
         n = 2 if k < 7 else 1
         return [(k, t) for t in split(-e, b, n) + split(ROWS - b, ROWS + e, n)]
 
+    def copies11(c, rows):
+        made = []
+        for lane, to in enumerate(('outer', 'inner')):
+            slot = jnp.where(even, 1 - lane, lane)
+            made.append((pltpu.make_async_remote_copy(
+                src_ref=u11.at[rows], dst_ref=v11.at[slot, rows], send_sem=s11.at[c, lane], recv_sem=r11.at[c, lane],
+                device_id={'sp': device[to]}, device_id_type=MESH), to))
+        return made
+
+    def send11(p, n):
+        for q in range(p, p + n, CHUNK):
+            row = from_inner(q, CHUNK)
+            for cp, to in copies11(row // CHUNK, pl.ds(row, CHUNK)):
+                start(cp, to)
+
     own_x.wait()
     h0[pl.ds(PAD, ROWS), :] = xb[pl.ds(EXT, ROWS), :].astype(jnp.float32)
-    run(interior(0) + interior(1))
+    run([task for k in range(EARLY) for task in interior(k)])
     arrived(x_halo)
     h0[pl.ds(16, EXT), :] = xb[pl.ds(0, EXT), :].astype(jnp.float32)
     h0[pl.ds(PAD + ROWS, EXT), :] = xb[pl.ds(EXT + ROWS, EXT), :].astype(jnp.float32)
@@ -232,7 +246,7 @@
 
     o8 = halo(u8, 256, 'outer', 1792, 256)
     i8 = halo(u8, 256, 'inner', 0, 256)
-    run([task for k in range(2, 8) for task in interior(k)])
+    run([task for k in range(EARLY, 8) for task in interior(k)])
 
     arrived([i8, o8])
     run([(8, side(1536, 512)), (8, side(0, 512))])
@@ -245,6 +259,9 @@
     arrived([i9])
     run([(9, side(0, 512))])
     i10b = halo(u10, 1024, 'inner', 0, 512)
+    arrived([i10a])
+    run([(10, side(0, 512))])
+    send11(0, 512)
     arrived([o9a])
     run([(9, side(1792, 256))])
     o10b = halo(u10, 1024, 'outer', 1792, 256)
@@ -252,26 +269,6 @@
     run([(9, side(1536, 256))])
     o10c = halo(u10, 1024, 'outer', 1536, 256)
 
-    weights(10)
-
-    def copies11(c, rows):
-        made = []
-        for lane, to in enumerate(('outer', 'inner')):
-            slot = jnp.where(even, 1 - lane, lane)
-            made.append((pltpu.make_async_remote_copy(
-                src_ref=u11.at[rows], dst_ref=v11.at[slot, rows], send_sem=s11.at[c, lane], recv_sem=r11.at[c, lane],
-                device_id={'sp': device[to]}, device_id_type=MESH), to))
-        return made
-
-    def send11(p, n):
-        for q in range(p, p + n, CHUNK):
-            row = from_inner(q, CHUNK)
-            for cp, to in copies11(row // CHUNK, pl.ds(row, CHUNK)):
-                start(cp, to)
-
-    arrived([i10a])
-    run([(10, side(0, 512))])
-    send11(0, 512)
     arrived([i10b])
     run([(10, side(512, 512))])
     send11(512, 512)
@@ -298,28 +295,32 @@
         c12[c] = [remote(u12.at[rows], v12r.at[rows], -2), remote(u12.at[rows], v12l.at[rows], 2)]
 
     weights(12)
-    c13 = {}
+    c13, out = {}, []
+    at_end = jnp.logical_not(has_l2 & has_r2)
     for c in ORDER:
         rows = pl.ds(c * CHUNK, CHUNK)
         arrived(c12[c])
         taps = jnp.where(has_l2, v12l[rows, :], 0), jnp.where(has_r2, v12r[rows, :], 0)
         tile = [(c * CHUNK, CHUNK)]
         finish(12, tile, pre_act(12, tile, taps))
-        c13[c] = [remote(u13.at[rows], v13.at[rows], 'partner')]
-
-    weights(13)
-    out = []
-    for c in ORDER:
-        rows = pl.ds(c * CHUNK, CHUNK)
-        arrived(c13[c])
-        other = v13[rows, :]
-        taps = jnp.where(low, 0, other), jnp.where(low, other, 0)
-        tile = [(c * CHUNK, CHUNK)]
-        finish(13, tile, pre_act(13, tile, taps))
+        c13[c] = [remote(u13.at[rows], v13.at[rows], 'partner', now=False)]
+        if len(c13) <= AHEAD:
+            start(*c13[c][0])
+        else:
+            @pl.when(jnp.logical_not(at_end))
+            def _():
+                c13[c][0][0].start()
         for j, cp in enumerate([pltpu.make_async_copy(ha.at[pl.ds(PAD + c * CHUNK, CHUNK)], h_ref.at[0, rows], osem.at[c, 0]),
                                 pltpu.make_async_copy(sk.at[rows], s_ref.at[0, rows], osem.at[c, 1])]):
             cp.start()
             out.append(cp)
+
+    for i, c in enumerate(ORDER):
+        arrived(c13[c])
+        if i + AHEAD < len(ORDER):
+            @pl.when(at_end)
+            def _():
+                c13[ORDER[i + AHEAD]][0][0].start()
 
     for cp, to in sent + [pair for made in c11.values() for pair in made]:
         if have[to] is None:
@@ -332,6 +333,18 @@
         cp.wait()
 
 
+def last_layer(h_in, s_in, other_ref, win, wres, wskip, h_out, s_out):
+    low = lax.axis_index('sp') < N_DEV // 2
+    cur, other = h_in[0], other_ref[...]
+    lhs = jnp.concatenate([jnp.where(low, 0, other), cur.astype(jnp.bfloat16), jnp.where(low, other, 0)], axis=1)
+    z = jnp.dot(lhs, win[0], preferred_element_type=jnp.float32)
+    gate = (jnp.tanh(z[:, :CH]) * jax.nn.sigmoid(z[:, CH:])).astype(jnp.bfloat16)
+    y = jnp.dot(gate, jnp.concatenate([wres[0], wskip[0]], axis=1), preferred_element_type=jnp.float32)
+    h_out[0] = cur + y[:, :CH]
+    s_out[0] = s_in[0] + y[:, CH:]
+
+
+LAST_ROWS = 1024
 N_REMOTE = 2 + 2 + 3 + 5 + 16 + 8
 
 
@@ -342,23 +355,35 @@
     def local_stack(x, w_in, w_res, w_skip):
         any_spec = pl.BlockSpec(memory_space=pl.ANY)
         u_big = [pltpu.VMEM((ROWS + 2 * EXT, CH), bf)] * 4
-        return pl.pallas_call(
+        wide = w_in.reshape(14, 3 * CH, 2 * CH)
+        h13, s13, other = pl.pallas_call(
             kernel,
-            out_shape=(jax.ShapeDtypeStruct(x.shape, f32), jax.ShapeDtypeStruct(x.shape, f32)),
+            out_shape=(jax.ShapeDtypeStruct(x.shape, f32), jax.ShapeDtypeStruct(x.shape, f32), jax.ShapeDtypeStruct((ROWS, CH), bf)),
             in_specs=[any_spec] * 4,
-            out_specs=(any_spec, any_spec),
+            out_specs=(any_spec, any_spec, any_spec),
             scratch_shapes=[
                 pltpu.VMEM((ROWS + 2 * EXT, CH), bf),
                 *[pltpu.VMEM((ROWS + 2 * PAD, CH), f32)] * 5, pltpu.VMEM((ROWS, CH), f32),
                 *u_big,
                 pltpu.VMEM((ROWS + 512, CH), bf), pltpu.VMEM((ROWS + 1024, CH), bf), pltpu.VMEM((ROWS + 2048, CH), bf),
-                *[pltpu.VMEM((ROWS, CH), bf)] * 3, pltpu.VMEM((2, ROWS, CH), bf), *[pltpu.VMEM((ROWS, CH), bf)] * 3,
-                pltpu.VMEM((14, 3 * CH, 2 * CH), bf), pltpu.VMEM((14, CH, 2 * CH), bf),
-                pltpu.SemaphoreType.DMA, pltpu.SemaphoreType.DMA((14, 3)), pltpu.SemaphoreType.DMA((8, 2)),
+                *[pltpu.VMEM((ROWS, CH), bf)] * 3, pltpu.VMEM((2, ROWS, CH), bf), *[pltpu.VMEM((ROWS, CH), bf)] * 2,
+                pltpu.VMEM((13, 3 * CH, 2 * CH), bf), pltpu.VMEM((13, CH, 2 * CH), bf),
+                pltpu.SemaphoreType.DMA, pltpu.SemaphoreType.DMA((13, 3)), pltpu.SemaphoreType.DMA((8, 2)),
                 pltpu.SemaphoreType.DMA((N_REMOTE,)), pltpu.SemaphoreType.DMA((N_REMOTE,)),
                 pltpu.SemaphoreType.DMA((8, 2)), pltpu.SemaphoreType.DMA((8, 2)),
             ],
             compiler_params=pltpu.CompilerParams(collective_id=0, has_side_effects=True, vmem_limit_bytes=56 * 1024 * 1024),
-        )(x, w_in.reshape(14, 3 * CH, 2 * CH), w_res, w_skip)
+        )(x, wide, w_res, w_skip)
+        rows = pl.BlockSpec((1, LAST_ROWS, CH), lambda i: (0, i, 0))
+        return pl.pallas_call(
+            last_layer,
+            grid=(ROWS // LAST_ROWS,),
+            out_shape=(jax.ShapeDtypeStruct(x.shape, f32), jax.ShapeDtypeStruct(x.shape, f32)),
+            in_specs=[rows, rows, pl.BlockSpec((LAST_ROWS, CH), lambda i: (i, 0)),
+                      pl.BlockSpec((1, 3 * CH, 2 * CH), lambda i: (13, 0, 0)),
+                      pl.BlockSpec((1, CH, CH), lambda i: (13, 0, 0)), pl.BlockSpec((1, CH, CH), lambda i: (13, 0, 0))],
+            out_specs=(rows, rows),
+            compiler_params=pltpu.CompilerParams(vmem_limit_bytes=60 * 1024 * 1024),
+        )(h13, s13, other, wide, w_res, w_skip)
 
     return jax.shard_map(local_stack, mesh=mesh, in_specs=(act_spec, P(), P(), P()), out_specs=(act_spec, act_spec), check_vma=False)

time: 70 us -> 68.2 us (0.974)
  local copies, waits for them, and re-layouts: 3.32 us -> 0 us
  Pallas kernels: 65.9 us -> 67.4 us
    pallas_call x0 -> x1, Pallas kernels: none -> 4.17 us  [local_stack(): pl.pallas_call(last_layer, grid=(ROWS // LAST_ROWS,), out_shape=(jax.Shap...]
    unnamed x4 -> x0, local copies, waits for them, and re-layouts: 3.32 us -> none
    pallas_call x1, Pallas kernels: 65.9 us -> 63.3 us  [local_stack(): pl.pallas_call(kernel, out_shape=(jax.ShapeDtypeStruct(x.shape, f32), jax...]
where the time goes in v5:
time: 68.2 us; the launch traced here: 68.1 us
  Pallas kernels  67.4 us (99%)
    pallas_call x1, Pallas kernels, local_stack(): pl.pallas_call(kernel, out_shape=(jax.ShapeDtypeStruct(x.shape, f32), jax...  63.3 us
    pallas_call x1, Pallas kernels, local_stack(): pl.pallas_call(last_layer, grid=(ROWS // LAST_ROWS,), out_shape=(jax.Shap...  4.17 us

profile of v5, /device:TPU:1, one launch (start us, length us, event | category | flops | bytes accessed | tf_op | source)
XLA Modules:
  0.0 68.1 jit_solution(11752674339293326725)
XLA Ops:
  0.6 63.3 %shard_map.59 = (f32[1,2048,128]{2,1,0:T(8,128)}, f32[1,2048,128]{2,1,0:T(8,128)}, bf16[2048,128]{1,0:T(8,128)(2,1)}) custom-call(bf16[1,2048,128]{2,1,0:T(8,128)(2,1)} %x_ref.1, bf16[14,384,256]{2,1,0:T(8,128)(2,1)} %bitcast.1, bf16[14,128,128]{2,1,0:T(8,128)(2,1)} %wres.1, bf16[14,128,128]{2,1,0:T(8,128)(2,1)} %wskip.1), custom_call_target="tpu_custom_call" | custom-call | tf_op jit(solution)/shard_map/pallas_call | solution.py:359
  63.9 4.2 %shard_map.60 = (f32[1,2048,128]{2,1,0:T(8,128)}, f32[1,2048,128]{2,1,0:T(8,128)}) custom-call(f32[1,2048,128]{2,1,0:T(8,128)} %get-tuple-element.5.h_in, f32[1,2048,128]{2,1,0:T(8,128)} %get-tuple-element.6.s_in, bf16[2048,128]{1,0:T(8,128)(2,1)} %get-tuple-element.7.other_ref, bf16[14,384,256]{2,1,0:T(8,128)(2,1)} %bitcast.2, bf16[14,128,128]{2,1,0:T(8,128)(2,1)} %wres.1, ...), custom_call_target="tpu_custom_call" | custom-call | tf_op jit(solution)/shard_map/pallas_call | solution.py:378

commit v6 on v5

--- a/solution.py
+++ b/solution.py
@@ -296,7 +296,7 @@
 
     weights(12)
     c13, out = {}, []
-    at_end = jnp.logical_not(has_l2 & has_r2)
+    at_end = jnp.logical_not(has_r2)
     for c in ORDER:
         rows = pl.ds(c * CHUNK, CHUNK)
         arrived(c12[c])
@@ -335,13 +335,21 @@
 
 def last_layer(h_in, s_in, other_ref, win, wres, wskip, h_out, s_out):
     low = lax.axis_index('sp') < N_DEV // 2
-    cur, other = h_in[0], other_ref[...]
-    lhs = jnp.concatenate([jnp.where(low, 0, other), cur.astype(jnp.bfloat16), jnp.where(low, other, 0)], axis=1)
-    z = jnp.dot(lhs, win[0], preferred_element_type=jnp.float32)
-    gate = (jnp.tanh(z[:, :CH]) * jax.nn.sigmoid(z[:, CH:])).astype(jnp.bfloat16)
-    y = jnp.dot(gate, jnp.concatenate([wres[0], wskip[0]], axis=1), preferred_element_type=jnp.float32)
-    h_out[0] = cur + y[:, :CH]
-    s_out[0] = s_in[0] + y[:, CH:]
+    taps = win[0, pl.ds(pl.multiple_of(jnp.where(low, CH, 0), CH), 2 * CH), :]
+    out_w = jnp.concatenate([wres[0], wskip[0]], axis=1)
+    parts = [pl.ds(i * 512, 512) for i in range(LAST_ROWS // 512)]
+
+    def pre_act(r):
+        cur, other = h_in[0, r, :].astype(jnp.bfloat16), other_ref[r, :]
+        lhs = jnp.concatenate([jnp.where(low, cur, other), jnp.where(low, other, cur)], axis=1)
+        return jnp.dot(lhs, taps, preferred_element_type=jnp.float32)
+
+    z = [pre_act(r) for r in parts]
+    for r, zr in zip(parts, z):
+        gate = (jnp.tanh(zr[:, :CH]) * jax.nn.sigmoid(zr[:, CH:])).astype(jnp.bfloat16)
+        y = jnp.dot(gate, out_w, preferred_element_type=jnp.float32)
+        h_out[0, r, :] = h_in[0, r, :] + y[:, :CH]
+        s_out[0, r, :] = s_in[0, r, :] + y[:, CH:]
 
 
 LAST_ROWS = 1024

time: 68.2 us -> 66.8 us (0.979)
  the two profiles are of different devices: /device:TPU:1 before, /device:TPU:5 now
where the time goes in v6:
time: 66.8 us; the launch traced here: 66.7 us
  Pallas kernels  66 us (99%)
    pallas_call x1, Pallas kernels, local_stack(): pl.pallas_call(kernel, out_shape=(jax.ShapeDtypeStruct(x.shape, f32), jax...  62.6 us
    pallas_call x1, Pallas kernels, local_stack(): pl.pallas_call(last_layer, grid=(ROWS // LAST_ROWS,), out_shape=(jax.Shap...  3.43 us

profile of v6, /device:TPU:5, one launch (start us, length us, event | category | flops | bytes accessed | tf_op | source)
XLA Modules:
  0.0 66.7 jit_solution(5992782083958427995)
XLA Ops:
  0.6 62.6 %shard_map.59 = (f32[1,2048,128]{2,1,0:T(8,128)}, f32[1,2048,128]{2,1,0:T(8,128)}, bf16[2048,128]{1,0:T(8,128)(2,1)}) custom-call(bf16[1,2048,128]{2,1,0:T(8,128)(2,1)} %x_ref.1, bf16[14,384,256]{2,1,0:T(8,128)(2,1)} %bitcast.1, bf16[14,128,128]{2,1,0:T(8,128)(2,1)} %wres.1, bf16[14,128,128]{2,1,0:T(8,128)(2,1)} %wskip.1), custom_call_target="tpu_custom_call" | custom-call | tf_op jit(solution)/shard_map/pallas_call | solution.py:367
  63.3 3.4 %shard_map.60 = (f32[1,2048,128]{2,1,0:T(8,128)}, f32[1,2048,128]{2,1,0:T(8,128)}) custom-call(f32[1,2048,128]{2,1,0:T(8,128)} %get-tuple-element.5.h_in, f32[1,2048,128]{2,1,0:T(8,128)} %get-tuple-element.6.s_in, bf16[2048,128]{1,0:T(8,128)(2,1)} %get-tuple-element.7.other_ref, bf16[14,384,256]{2,1,0:T(8,128)(2,1)} %bitcast.2, bf16[14,128,128]{2,1,0:T(8,128)(2,1)} %wres.1, ...), custom_call_target="tpu_custom_call" | custom-call | tf_op jit(solution)/shard_map/pallas_call | solution.py:386

commit v7 on v6

--- a/solution.py
+++ b/solution.py
@@ -15,7 +15,7 @@
 PAD = EXT + 16
 REACH = [256, 256, 256, 240, 224, 192, 128, 0]
 CHUNK = 256
-AHEAD = 3
+AHEAD = (5, 3)
 BAND = [496, 512, 512, 496, 480, 448, 384, 256]
 EARLY = 2
 ORDER = [1, 6, 0, 7, 3, 4, 2, 5]
@@ -296,7 +296,7 @@
 
     weights(12)
     c13, out = {}, []
-    at_end = jnp.logical_not(has_r2)
+    ends = (jnp.logical_not(has_l2), jnp.logical_not(has_r2))
     for c in ORDER:
         rows = pl.ds(c * CHUNK, CHUNK)
         arrived(c12[c])
@@ -304,12 +304,13 @@
         tile = [(c * CHUNK, CHUNK)]
         finish(12, tile, pre_act(12, tile, taps))
         c13[c] = [remote(u13.at[rows], v13.at[rows], 'partner', now=False)]
-        if len(c13) <= AHEAD:
-            start(*c13[c][0])
-        else:
-            @pl.when(jnp.logical_not(at_end))
+        waits = [end for end, ahead in zip(ends, AHEAD) if len(c13) > ahead]
+        if waits:
+            @pl.when(jnp.logical_not(functools.reduce(jnp.logical_or, waits)))
             def _():
                 c13[c][0][0].start()
+        else:
+            start(*c13[c][0])
         for j, cp in enumerate([pltpu.make_async_copy(ha.at[pl.ds(PAD + c * CHUNK, CHUNK)], h_ref.at[0, rows], osem.at[c, 0]),
                                 pltpu.make_async_copy(sk.at[rows], s_ref.at[0, rows], osem.at[c, 1])]):
             cp.start()
@@ -317,10 +318,11 @@
 
     for i, c in enumerate(ORDER):
         arrived(c13[c])
-        if i + AHEAD < len(ORDER):
-            @pl.when(at_end)
-            def _():
-                c13[ORDER[i + AHEAD]][0][0].start()
+        for end, ahead in zip(ends, AHEAD):
+            if i + ahead < len(ORDER):
+                @pl.when(end)
+                def _():
+                    c13[ORDER[i + ahead]][0][0].start()
 
     for cp, to in sent + [pair for made in c11.values() for pair in made]:
         if have[to] is None:

time: 66.8 us -> 66.1 us (0.990)
  the two profiles are of different devices: /device:TPU:5 before, /device:TPU:9 now
where the time goes in v7:
time: 66.1 us; the launch traced here: 65.9 us
  Pallas kernels  65.3 us (99%)
    pallas_call x1, Pallas kernels, local_stack(): pl.pallas_call(kernel, out_shape=(jax.ShapeDtypeStruct(x.shape, f32), jax...  61.8 us
    pallas_call x1, Pallas kernels, local_stack(): pl.pallas_call(last_layer, grid=(ROWS // LAST_ROWS,), out_shape=(jax.Shap...  3.43 us

profile of v7, /device:TPU:9, one launch (start us, length us, event | category | flops | bytes accessed | tf_op | source)
XLA Modules:
  0.0 65.9 jit_solution(2836363182631441324)
XLA Ops:
  0.6 61.8 %shard_map.59 = (f32[1,2048,128]{2,1,0:T(8,128)}, f32[1,2048,128]{2,1,0:T(8,128)}, bf16[2048,128]{1,0:T(8,128)(2,1)}) custom-call(bf16[1,2048,128]{2,1,0:T(8,128)(2,1)} %x_ref.1, bf16[14,384,256]{2,1,0:T(8,128)(2,1)} %bitcast.1, bf16[14,128,128]{2,1,0:T(8,128)(2,1)} %wres.1, bf16[14,128,128]{2,1,0:T(8,128)(2,1)} %wskip.1), custom_call_target="tpu_custom_call" | custom-call | tf_op jit(solution)/shard_map/pallas_call | solution.py:369
  62.5 3.4 %shard_map.60 = (f32[1,2048,128]{2,1,0:T(8,128)}, f32[1,2048,128]{2,1,0:T(8,128)}) custom-call(f32[1,2048,128]{2,1,0:T(8,128)} %get-tuple-element.5.h_in, f32[1,2048,128]{2,1,0:T(8,128)} %get-tuple-element.6.s_in, bf16[2048,128]{1,0:T(8,128)(2,1)} %get-tuple-element.7.other_ref, bf16[14,384,256]{2,1,0:T(8,128)(2,1)} %bitcast.2, bf16[14,128,128]{2,1,0:T(8,128)(2,1)} %wres.1, ...), custom_call_target="tpu_custom_call" | custom-call | tf_op jit(solution)/shard_map/pallas_call | solution.py:388

commit v8 on v7

--- a/solution.py
+++ b/solution.py
@@ -15,7 +15,7 @@
 PAD = EXT + 16
 REACH = [256, 256, 256, 240, 224, 192, 128, 0]
 CHUNK = 256
-AHEAD = (5, 3)
+AHEAD = (4, 3)
 BAND = [496, 512, 512, 496, 480, 448, 384, 256]
 EARLY = 2
 ORDER = [1, 6, 0, 7, 3, 4, 2, 5]

time: 66.1 us -> 67.5 us (1.021)
  the two profiles are of different devices: /device:TPU:9 before, /device:TPU:1 now
where the time goes in v8:
time: 67.5 us; the launch traced here: 67.4 us
  Pallas kernels  66.7 us (99%)
    pallas_call x1, Pallas kernels, local_stack(): pl.pallas_call(kernel, out_shape=(jax.ShapeDtypeStruct(x.shape, f32), jax...  63.3 us
    pallas_call x1, Pallas kernels, local_stack(): pl.pallas_call(last_layer, grid=(ROWS // LAST_ROWS,), out_shape=(jax.Shap...  3.43 us

profile of v8, /device:TPU:1, one launch (start us, length us, event | category | flops | bytes accessed | tf_op | source)
XLA Modules:
  0.0 67.4 jit_solution(15544208905721939811)
XLA Ops:
  0.6 63.3 %shard_map.59 = (f32[1,2048,128]{2,1,0:T(8,128)}, f32[1,2048,128]{2,1,0:T(8,128)}, bf16[2048,128]{1,0:T(8,128)(2,1)}) custom-call(bf16[1,2048,128]{2,1,0:T(8,128)(2,1)} %x_ref.1, bf16[14,384,256]{2,1,0:T(8,128)(2,1)} %bitcast.1, bf16[14,128,128]{2,1,0:T(8,128)(2,1)} %wres.1, bf16[14,128,128]{2,1,0:T(8,128)(2,1)} %wskip.1), custom_call_target="tpu_custom_call" | custom-call | tf_op jit(solution)/shard_map/pallas_call | solution.py:369
  64.0 3.4 %shard_map.60 = (f32[1,2048,128]{2,1,0:T(8,128)}, f32[1,2048,128]{2,1,0:T(8,128)}) custom-call(f32[1,2048,128]{2,1,0:T(8,128)} %get-tuple-element.5.h_in, f32[1,2048,128]{2,1,0:T(8,128)} %get-tuple-element.6.s_in, bf16[2048,128]{1,0:T(8,128)(2,1)} %get-tuple-element.7.other_ref, bf16[14,384,256]{2,1,0:T(8,128)(2,1)} %bitcast.2, bf16[14,128,128]{2,1,0:T(8,128)(2,1)} %wres.1, ...), custom_call_target="tpu_custom_call" | custom-call | tf_op jit(solution)/shard_map/pallas_call | solution.py:388
